TPU v7x, 32 devices: a 4x4x1 block of a 4x4x8 slice. The times are simulated.
32 devices in a mesh: dp: 1 (over z), tp: 32 (over y, x, core).
Axes of the slice: x: 4, y: 4, z: 1, core: 2. Of those that a mesh axis runs over, the one named last changes fastest.
The devices are a block of a 4x4x8 slice.
Arguments:
- act_in: bfloat16 [32, 128, 4096], P('dp')
- ln_gain: float32 [2, 4096], replicated
- ln_bias: float32 [2, 4096], replicated
- w_qkv: bfloat16 [2, 4096, 32, 384], P(None, None, 'tp')
- w_out: bfloat16 [2, 4096, 4096], P(None, 'tp')
- w_up: bfloat16 [2, 4096, 16384], P(None, None, 'tp')
- w_down: bfloat16 [2, 16384, 4096], P(None, 'tp')
Outputs:
- output: bfloat16 [32, 128, 4096], P('dp')
All inputs are finite; a program needn't handle non-finite values.
Results may differ from a plain program's by a relative error of at most 0.02.
Values are sent between devices in bfloat16 or wider.
A program may use at most 768 MiB of HBM per device.

v0:
```python
import jax
import jax.numpy as jnp
from jax import lax
from jax.sharding import PartitionSpec as P

LN_EPS = 1e-5
ROPE_BASE = 10000.0


def layer_norm(hidden, gain, bias):
    hidden_f = hidden.astype(jnp.float32)
    row_mean = jnp.mean(hidden_f, axis=-1, keepdims=True)
    centered = hidden_f - row_mean
    row_var = jnp.mean(centered * centered, axis=-1, keepdims=True)
    return (centered * lax.rsqrt(row_var + LN_EPS) * gain + bias).astype(jnp.bfloat16)


def rope_tables(seq_len, head_dim):
    half_dim = head_dim // 2
    inv_freq = ROPE_BASE ** (-2.0 * jnp.arange(half_dim, dtype=jnp.float32) / head_dim)
    angles = jnp.arange(seq_len, dtype=jnp.float32)[:, None] * inv_freq[None, :]
    return jnp.cos(angles), jnp.sin(angles)


def apply_rope(proj, cos_tab, sin_tab):
    half_dim = proj.shape[-1] // 2
    first = proj[..., :half_dim]
    second = proj[..., half_dim:]
    return jnp.concatenate([first * cos_tab - second * sin_tab, second * cos_tab + first * sin_tab], axis=-1)


def layer_partial(hidden, gain, bias, w_qkv, w_out, w_up, w_down):
    batch, seq_len, d_model = hidden.shape
    groups = w_qkv.shape[1]
    attn_width = w_out.shape[0]
    head_dim = (w_qkv.shape[2] - attn_width // groups) // 2
    group_heads = attn_width // (groups * head_dim)
    normed = layer_norm(hidden, gain, bias)
    qkv_proj = jnp.einsum("bsd,dgc->bsgc", normed, w_qkv, preferred_element_type=jnp.float32)
    qkv_proj = qkv_proj.reshape(batch, seq_len, groups, group_heads + 2, head_dim)
    cos_tab, sin_tab = rope_tables(seq_len, head_dim)
    query = apply_rope(qkv_proj[:, :, :, :group_heads], cos_tab[None, :, None, None, :], sin_tab[None, :, None, None, :]).astype(jnp.bfloat16)
    keys = apply_rope(qkv_proj[:, :, :, group_heads], cos_tab[None, :, None, :], sin_tab[None, :, None, :]).astype(jnp.bfloat16)
    values = qkv_proj[:, :, :, group_heads + 1].astype(jnp.bfloat16)
    scores = jnp.einsum("bsgrd,btgd->bgrst", query, keys, preferred_element_type=jnp.float32) * (head_dim ** -0.5)
    positions = jnp.arange(seq_len)
    allowed = positions[:, None] >= positions[None, :]
    scores = jnp.where(allowed, scores, -1e30)
    attn_probs = jax.nn.softmax(scores, axis=-1).astype(jnp.bfloat16)
    context = jnp.einsum("bgrst,btgd->bgrsd", attn_probs, values, preferred_element_type=jnp.float32).astype(jnp.bfloat16)
    out_heads = w_out.reshape(groups, group_heads, head_dim, d_model)
    attn_part = jnp.einsum("bgrsd,grde->bse", context, out_heads, preferred_element_type=jnp.float32)
    up_proj = jnp.einsum("bsd,df->bsf", normed, w_up, preferred_element_type=jnp.float32)
    gelu_out = jax.nn.gelu(up_proj, approximate=False).astype(jnp.bfloat16)
    mlp_part = jnp.einsum("bsf,fe->bse", gelu_out, w_down, preferred_element_type=jnp.float32)
    return attn_part + mlp_part


def solution(mesh):
    def shard_body(act_in, ln_gain, ln_bias, w_qkv, w_out, w_up, w_down):
        hidden = act_in
        for layer_idx in range(ln_gain.shape[0]):
            local_sum = layer_partial(hidden, ln_gain[layer_idx], ln_bias[layer_idx], w_qkv[layer_idx], w_out[layer_idx], w_up[layer_idx], w_down[layer_idx]).astype(jnp.bfloat16)
            reduced = lax.psum(local_sum, "tp")
            hidden = (hidden.astype(jnp.float32) + reduced.astype(jnp.float32)).astype(jnp.bfloat16)
        return hidden

    return jax.shard_map(shard_body, mesh=mesh, in_specs=(P("dp", None, None), P(None, None), P(None, None), P(None, None, "tp", None), P(None, "tp", None), P(None, None, "tp"), P(None, "tp", None)), out_specs=P("dp", None, None), check_vma=False)
```

profile of v0, /device:TPU:97, one launch (start us, length us, event | category | flops | bytes accessed | tf_op | source)
XLA Modules:
  0.0 869.2 jit_solution(14083610386789003931)
XLA Ops:
  6.6 11.4 %convert_reduce_fusion.1 = f32[32,128]{1,0:T(8,128)S(1)} fusion(bf16[32,128,4096]{2,1,0:T(8,128)(2,1)} %param.7), kind=kLoop, calls=%fused_computation.5 | loop fusion | flops 33550336 | bytes 33570816 | tf_op jit(solution)/shard_map/reduce_sum | solution.py:12
  18.0 13.0 %fusion.8 = f32[32,128]{1,0:T(8,128)S(1)} fusion(bf16[32,128,4096]{2,1,0:T(8,128)(2,1)} %param.7, f32[32,128]{1,0:T(8,128)S(1)} %broadcast_multiply_fusion.1), kind=kLoop, calls=%fused_computation.14 | loop fusion | flops 67104768 | bytes 33587200 | tf_op jit(solution)/shard_map/reduce_sum | solution.py:14
  31.1 0.6 fusion.236
  31.7 0.6 fusion.237
  32.6 2.3 slice_bitcast_fusion
  34.8 2.8 copy.8
  37.7 19.1 %fusion.121 = f32[32,128,1,3,128]{1,4,3,0,2:T(8,128)S(1)} fusion(bf16[3,128,4096,1]{2,1,0,3:T(8,128)(2,1)} %bitcast.151, f32[4096]{0:T(1024)S(1)} %bitcast.158, f32[4096]{0:T(1024)S(1)} %bitcast.156, f32[32,128]{1,0:T(8,128)S(1)} %add_rsqrt_fusion.1, f32[32,128]{1,0:T(8,128)S(1)} %broadcast_multiply_fusion.1, bf16[32,128,4096]{2,1,0:T(8,128)(2,1)} %param.7), kind=kOutput, calls=%fused_computation.148 | convolution fusion | flops 12985565184 | bytes 43057152 | tf_op jit(solution)/shard_map/bsd,dgc->bsgc/dot_general | solution.py:39
  56.8 0.2 fusion.168
  57.0 0.2 fusion.167
  57.2 2.2 copy-done.1
  59.7 0.3 fusion.161
  60.1 26.0 %convert_reduce_fusion.5 = (u32[128,512]{1,0:T(8,128)S(1)}, u32[128,512]{1,0:T(8,128)}, f32[32,128,512]{2,1,0:T(8,128)}) fusion(bf16[2,4096,512]{2,1,0:T(8,128)(2,1)S(1)} %bitcast.161, bf16[32,128,4096]{2,1,0:T(8,128)(2,1)} %param.7, f32[4096]{0:T(1024)S(1)} %bitcast.159, f32[4096]{0:T(1024)S(1)} %bitcast.157, f32[32,128]{1,0:T(8,128)S(1)} %add_rsqrt_fusion.1, ...), kind=kOutput, calls=%fused_computation.44 | convolution fusion | flops 17303470080 | bytes 46727168 | tf_op jit(solution)/shard_map/bsd,df->bsf/dot_general | solution.py:53
  86.1 0.6 fusion.238
  86.6 0.3 fusion.124
  87.0 26.0 %fusion.126 = f32[32,128,4096]{2,1,0:T(8,128)} fusion(f32[32,128,1,3,128]{1,4,3,0,2:T(8,128)} %copy-done.1, bf16[2,128,4096]{2,1,0:T(8,128)(2,1)} %param.11, f32[32,1,1,128,128]{3,4,0,2,1:T(8,128)S(1)} %get-tuple-element.26, f32[32,128]{1,0:T(8,128)S(1)} %fusion.124, f32[32,128]{1,0:T(8,128)S(1)} %get-tuple-element.25), kind=kOutput, calls=%fused_computation.163 | convolution fusion | flops 4431282176 | bytes 71335936 | tf_op jit(solution)/shard_map/bgrsd,grde->bse/dot_general | solution.py:52
  113.0 46.5 %add_convert_fusion.1 = bf16[32,128,4096]{2,1,0:T(8,128)(2,1)} fusion(f32[32,128,4096]{2,1,0:T(8,128)} %fusion.126, f32[32,128,512]{2,1,0:T(8,128)} %get-tuple-element.27, u32[128,512]{1,0:T(8,128)S(1)} %copy-done.14, u32[128,512]{1,0:T(8,128)S(1)} %get-tuple-element.7, bf16[2,512,4096]{2,1,0:T(8,128)(2,1)} %param.13), kind=kOutput, calls=%fused_computation.21 | convolution fusion | flops 17356029952 | bytes 113770496 | tf_op jit(solution)/shard_map/bsf,fe->bse/dot_general | solution.py:55
  159.7 1.8 copy-done
  161.5 3.1 copy.16
  164.6 248.4 %all-reduce.3.cloned.1.call-done = bf16[32,128,4096]{2,1,0:T(8,128)(2,1)} async-done(((bf16[32,128,4096]{2,1,0:T(8,128)(2,1)}), bf16[32,128,4096]{2,1,0:T(8,128)(2,1)}) %all-reduce.3.cloned.1.call-update) | async-done | bytes 33554448 | tf_op jit(solution)/shard_map/psum | solution.py:64
  413.0 33.2 %convert_reduce_fusion = (f32[32,128]{1,0:T(8,128)S(1)}, bf16[32,128,4096]{2,1,0:T(8,128)(2,1)}) fusion(bf16[32,128,4096]{2,1,0:T(8,128)(2,1)} %all-reduce.3.cloned.1.call-done, bf16[32,128,4096]{2,1,0:T(8,128)(2,1)} %param.7), kind=kLoop, calls=%fused_computation.2 | loop fusion | flops 100659200 | bytes 100679680 | tf_op jit(solution)/shard_map/reduce_sum | solution.py:12
  446.2 13.0 %fusion.4 = f32[32,128]{1,0:T(8,128)S(1)} fusion(bf16[32,128,4096]{2,1,0:T(8,128)(2,1)} %get-tuple-element.10, f32[32,128]{1,0:T(8,128)S(1)} %broadcast_multiply_fusion), kind=kLoop, calls=%fused_computation.10 | loop fusion | flops 67104768 | bytes 33587200 | tf_op jit(solution)/shard_map/reduce_sum | solution.py:14
  459.3 18.9 %fusion.118 = f32[32,128,1,3,128]{1,4,0,3,2:T(8,128)S(1)} fusion(bf16[3,128,4096,1]{2,1,3,0:T(8,128)(2,1)S(1)} %bitcast.150, f32[4096]{0:T(1024)S(1)} %bitcast.154, f32[4096]{0:T(1024)S(1)} %bitcast.152, f32[32,128]{1,0:T(8,128)S(1)} %add_rsqrt_fusion, f32[32,128]{1,0:T(8,128)S(1)} %broadcast_multiply_fusion, bf16[32,128,4096]{2,1,0:T(8,128)(2,1)} %get-tuple-element.10), kind=kOutput, calls=%fused_computation.147 | convolution fusion | flops 12985565184 | bytes 43057152 | tf_op jit(solution)/shard_map/bsd,dgc->bsgc/dot_general | solution.py:39
  478.2 0.3 fusion.165
  478.5 2.4 copy-done.2
  481.1 25.2 %convert_reduce_fusion.3 = (u32[128,512]{1,0:T(8,128)S(1)}, u32[128,512]{1,0:T(8,128)S(1)}, f32[32,128,512]{2,1,0:T(8,128)}) fusion(bf16[2,4096,512]{2,1,0:T(8,128)(2,1)S(1)} %bitcast.163, bf16[32,128,4096]{2,1,0:T(8,128)(2,1)} %get-tuple-element.10, f32[4096]{0:T(1024)S(1)} %bitcast.155, f32[4096]{0:T(1024)S(1)} %bitcast.153, ...), kind=kOutput, calls=%fused_computation.39 | convolution fusion | flops 17303470080 | bytes 46727168 | tf_op jit(solution)/shard_map/bsd,df->bsf/dot_general | solution.py:53
  506.3 0.3 fusion.163
  506.7 0.6 fusion.239
  507.2 0.3 fusion.125
  507.6 26.0 %fusion.127 = f32[32,128,4096]{2,1,0:T(8,128)} fusion(f32[32,128,1,3,128]{1,4,0,3,2:T(8,128)} %copy-done.2, bf16[2,128,4096]{2,1,0:T(8,128)(2,1)} %param.11, f32[32,1,1,128,128]{3,4,0,2,1:T(8,128)S(1)} %get-tuple-element.29, f32[32,128]{1,0:T(8,128)S(1)} %fusion.125, f32[32,128]{1,0:T(8,128)S(1)} %get-tuple-element.28), kind=kOutput, calls=%fused_computation.164 | convolution fusion | flops 4431282176 | bytes 71335936 | tf_op jit(solution)/shard_map/bgrsd,grde->bse/dot_general | solution.py:52
  533.6 45.9 %add_convert_fusion = bf16[32,128,4096]{2,1,0:T(8,128)(2,1)} fusion(f32[32,128,4096]{2,1,0:T(8,128)} %fusion.127, f32[32,128,512]{2,1,0:T(8,128)} %get-tuple-element.30, u32[128,512]{1,0:T(8,128)S(1)} %get-tuple-element.6, u32[128,512]{1,0:T(8,128)S(1)} %get-tuple-element.5, bf16[2,512,4096]{2,1,0:T(8,128)(2,1)} %param.13), kind=kOutput, calls=%fused_computation.20 | convolution fusion | flops 17356029952 | bytes 113770496 | tf_op jit(solution)/shard_map/bsf,fe->bse/dot_general | solution.py:55
  579.6 249.4 %all-reduce.5.cloned.1.call-done = bf16[32,128,4096]{2,1,0:T(8,128)(2,1)} async-done(((bf16[32,128,4096]{2,1,0:T(8,128)(2,1)}), bf16[32,128,4096]{2,1,0:T(8,128)(2,1)}) %all-reduce.5.cloned.1.call-update) | async-done | bytes 33554448 | tf_op jit(solution)/shard_map/psum | solution.py:64
  829.0 33.1 %fusion.13 = bf16[32,128,4096]{2,1,0:T(8,128)(2,1)} fusion(bf16[32,128,4096]{2,1,0:T(8,128)(2,1)} %get-tuple-element.10, bf16[32,128,4096]{2,1,0:T(8,128)(2,1)} %all-reduce.5.cloned.1.call-done), kind=kLoop, calls=%fused_computation.19 | loop fusion | flops 67108864 | bytes 100663296 | tf_op jit(solution)/shard_map/convert_element_type | solution.py:65
  (55 shorter events, 0.9 us)
Async XLA Ops:
  6.5 406.4 %all-reduce.3.cloned.1.call-start = ((), (), s32[]{:S(2)}) async-start(), calls=%async_computation | async-start | bytes 67108864 | tf_op jit(solution)/shard_map/psum | solution.py:64
  6.6 79.5 %copy-start.10 = (pred[128,128]{0,1:T(8,128)(4,1)}, pred[128,128]{0,1:T(8,128)(4,1)S(1)}, u32[]{:S(2)}) copy-start(pred[128,128]{0,1:T(8,128)(4,1)S(1)} %iota_compare_fusion) | copy-start | bytes 49156
  6.6 25.9 %slice-start = ((s8[6291456]{0:T(1024)(128)(4,1)}), s8[4194304]{0:T(1024)(128)(4,1)S(1)}, s32[]{:S(2)}) async-start(s8[6291456]{0:T(1024)(128)(4,1)} %bitcast.148), calls=%async_computation.2 | async-start | bytes 8388608
  18.0 13.1 %copy-start.8 = (f32[2,4096]{1,0:T(2,128)S(1)}, f32[2,4096]{1,0:T(2,128)}, u32[]{:S(2)}) copy-start(f32[2,4096]{1,0:T(2,128)} %param.8) | copy-start | bytes 98308
  18.0 13.7 %copy-start.9 = (f32[2,4096]{1,0:T(2,128)S(1)}, f32[2,4096]{1,0:T(2,128)}, u32[]{:S(2)}) copy-start(f32[2,4096]{1,0:T(2,128)} %param.9) | copy-start | bytes 98308
  18.0 14.5 %slice-start.1 = ((s8[6291456]{0:T(1024)(128)(4,1)}), s8[2097152]{0:T(1024)(128)(4,1)S(1)}, s32[]{:S(2)}) async-start(s8[6291456]{0:T(1024)(128)(4,1)} %bitcast.148), calls=%async_computation.3 | async-start | bytes 4194304
  32.5 27.2 %copy-start.4 = (f32[128,64]{0,1:T(8,128)}, f32[128,64]{0,1:T(8,128)S(1)}, u32[]{:S(2)}) copy-start(f32[128,64]{0,1:T(8,128)S(1)} %get-tuple-element.23) | copy-start | bytes 98308
  32.6 27.2 %copy-start.6 = (f32[128,64]{0,1:T(8,128)}, f32[128,64]{0,1:T(8,128)S(1)}, u32[]{:S(2)}) copy-start(f32[128,64]{0,1:T(8,128)S(1)} %get-tuple-element.24) | copy-start | bytes 98308
  37.7 22.3 %slice-start.2 = ((s8[8388608]{0:T(1024)(128)(4,1)}), s8[4194304]{0:T(1024)(128)(4,1)S(1)}, s32[]{:S(2)}) async-start(s8[8388608]{0:T(1024)(128)(4,1)} %bitcast.160), calls=%async_computation.4 | async-start | bytes 8388608
  37.7 22.3 %slice-start.3 = ((s8[8388608]{0:T(1024)(128)(4,1)}), s8[4194304]{0:T(1024)(128)(4,1)S(1)}, s32[]{:S(2)}) async-start(s8[8388608]{0:T(1024)(128)(4,1)} %bitcast.160), calls=%async_computation.5 | async-start | bytes 8388608
  56.8 2.7 copy-start.1
  87.0 26.0 %copy-start.14 = (u32[128,512]{1,0:T(8,128)S(1)}, u32[128,512]{1,0:T(8,128)}, u32[]{:S(2)}) copy-start(u32[128,512]{1,0:T(8,128)} %get-tuple-element.8) | copy-start | bytes 786436
  159.6 1.9 copy-start
  159.6 669.3 %all-reduce.5.cloned.1.call-start = ((), (), s32[]{:S(2)}) async-start(), calls=%async_computation.1 | async-start | bytes 67108864 | tf_op jit(solution)/shard_map/psum | solution.py:64
  446.1 13.1 %copy-start.3 = (bf16[384,4096]{1,0:T(8,128)(2,1)S(1)}, bf16[384,4096]{1,0:T(8,128)(2,1)}, u32[]{:S(2)}) copy-start(bf16[384,4096]{1,0:T(8,128)(2,1)} %copy.16) | copy-start | bytes 9437188
  446.2 13.1 %copy-start.12 = (f32[1,4096]{1,0:T(1,128)S(1)}, f32[1,4096]{1,0:T(1,128)}, u32[]{:S(2)}) copy-start(f32[1,4096]{1,0:T(1,128)} %get-tuple-element.19) | copy-start | bytes 49156
  446.2 13.1 %copy-start.13 = (f32[1,4096]{1,0:T(1,128)S(1)}, f32[1,4096]{1,0:T(1,128)}, u32[]{:S(2)}) copy-start(f32[1,4096]{1,0:T(1,128)} %get-tuple-element.21) | copy-start | bytes 49156
  446.2 34.9 %slice-start.4 = ((s8[8388608]{0:T(1024)(128)(4,1)}), s8[4194304]{0:T(1024)(128)(4,1)S(1)}, s32[]{:S(2)}) async-start(s8[8388608]{0:T(1024)(128)(4,1)} %bitcast.162), calls=%async_computation.6 | async-start | bytes 8388608
  459.3 18.9 %copy-start.5 = (f32[128,64]{0,1:T(8,128)S(1)}, f32[128,64]{0,1:T(8,128)}, u32[]{:S(2)}) copy-start(f32[128,64]{0,1:T(8,128)} %copy-done.4) | copy-start | bytes 98308
  459.3 18.9 %copy-start.7 = (f32[128,64]{0,1:T(8,128)S(1)}, f32[128,64]{0,1:T(8,128)}, u32[]{:S(2)}) copy-start(f32[128,64]{0,1:T(8,128)} %copy-done.6) | copy-start | bytes 98308
  459.3 21.8 %slice-start.5 = ((s8[8388608]{0:T(1024)(128)(4,1)}), s8[4194304]{0:T(1024)(128)(4,1)S(1)}, s32[]{:S(2)}) async-start(s8[8388608]{0:T(1024)(128)(4,1)} %bitcast.162), calls=%async_computation.7 | async-start | bytes 8388608
  478.2 2.7 copy-start.2
  481.1 25.6 %copy-start.11 = (pred[128,128]{0,1:T(8,128)(4,1)S(1)}, pred[128,128]{0,1:T(8,128)(4,1)}, u32[]{:S(2)}) copy-start(pred[128,128]{0,1:T(8,128)(4,1)} %copy-done.10) | copy-start | bytes 49156
Sparse Core Ops, SparseCore 0:
  159.8 253.1 all-reduce.2
  579.7 249.2 all-reduce.4
where the time goes:
time: 875 us; the launch traced here: 869 us
  waiting for transfers between devices  498 us (57%)
  matrix products  235 us (27%)
  other arithmetic  106 us (12%)
  local copies, waits for them, and re-layouts  16.3 us (2%)
  between operations  14.1 us (2%)
    psum x2, waiting for transfers between devices, shard_body(): reduced = lax.psum(local_sum, 'tp')  498 us
    dot_general x2, matrix products, layer_partial(): jnp.einsum('bsf,fe->bse', gelu_out, w_down, preferred_element_type=jnp.fl...  92.4 us
    dot_general x2, matrix products, layer_partial(): jnp.einsum('bgrsd,grde->bse', context, out_heads, preferred_element_type=...  52 us
    dot_general x2, matrix products, layer_partial(): jnp.einsum('bsd,df->bsf', normed, w_up, preferred_element_type=jnp.float32)  51.2 us
    reduce_sum x2, other arithmetic, layer_norm(): row_mean = jnp.mean(hidden_f, axis=-1, keepdims=True)  44.5 us
    dot_general x2, matrix products, layer_partial(): jnp.einsum('bsd,dgc->bsgc', normed, w_qkv, preferred_element_type=jnp.flo...  38 us
    convert_element_type x1, other arithmetic, shard_body(): (hidden.astype(jnp.float32) + reduced.astype(jnp.float32)).astype(jnp.bfl...  33.1 us
    reduce_sum x2, other arithmetic, layer_norm(): row_var = jnp.mean(centered * centered, axis=-1, keepdims=True)  26 us
  transfers between devices with their start and end apart: 2, of which 2 were waited for; matrix products, arithmetic and copies ran while one was open for 0% of the time, Pallas kernels for 0%

commit v1 on v0

v1 whole, which is shorter than its diff:
```python
import functools
import math

import jax
import jax.numpy as jnp
from jax import lax
from jax.experimental import pallas as pl
from jax.experimental.pallas import tpu as pltpu
from jax.sharding import PartitionSpec as P

LN_EPS = 1e-5
ROPE_BASE = 10000.0
CORES = 2
RINGS = 4
MESH_ID = pl.DeviceIdType.MESH
BF16 = jnp.bfloat16
F32 = jnp.float32
VMEM_LIMIT = 66_000_000


def layer_norm(hidden, gain, bias):
    hidden_f = hidden.astype(F32)
    row_mean = jnp.mean(hidden_f, axis=-1, keepdims=True)
    centered = hidden_f - row_mean
    row_var = jnp.mean(centered * centered, axis=-1, keepdims=True)
    return (centered * lax.rsqrt(row_var + LN_EPS) * gain + bias).astype(BF16)


def rope_tables(seq_len, head_dim):
    half_dim = head_dim // 2
    inv_freq = ROPE_BASE ** (-2.0 * jnp.arange(half_dim, dtype=F32) / head_dim)
    angles = jnp.arange(seq_len, dtype=F32)[:, None] * inv_freq[None, :]
    return jnp.cos(angles), jnp.sin(angles)


def apply_rope(proj, cos_tab, sin_tab):
    half_dim = proj.shape[-1] // 2
    first = proj[..., :half_dim]
    second = proj[..., half_dim:]
    return jnp.concatenate([first * cos_tab - second * sin_tab, second * cos_tab + first * sin_tab], axis=-1)


def attend(qkv, head_dim):
    seq_len = qkv.shape[1]
    cos_tab, sin_tab = rope_tables(seq_len, head_dim)
    query = apply_rope(qkv[..., :head_dim], cos_tab, sin_tab).astype(BF16)
    keys = apply_rope(qkv[..., head_dim:2 * head_dim], cos_tab, sin_tab).astype(BF16)
    values = qkv[..., 2 * head_dim:].astype(BF16)
    scores = jnp.einsum("bsd,btd->bst", query, keys, preferred_element_type=F32) * (head_dim ** -0.5)
    positions = jnp.arange(seq_len)
    scores = jnp.where(positions[:, None] >= positions[None, :], scores, -1e30)
    probs = jax.nn.softmax(scores, axis=-1).astype(BF16)
    return jnp.einsum("bst,btd->bsd", probs, values, preferred_element_type=F32).astype(BF16)


class Torus:
    def __init__(self, side):
        self.side = side
        self.chips = side * side

    def me(self):
        idx = lax.axis_index("tp")
        core = lax.rem(idx, CORES)
        chip = lax.div(idx, CORES)
        return core, lax.rem(chip, self.side), lax.div(chip, self.side)

    def position(self, ring, x, y):
        major = y if ring < 2 else x
        return self.side * major + lax.rem(x + y, self.side)

    def chip_at(self, ring, pos):
        pos = lax.rem(pos + 2 * self.chips, self.chips)
        major = lax.div(pos, self.side)
        minor = lax.rem(lax.rem(pos, self.side) - major + self.side, self.side)
        return major * self.side + minor if ring < 2 else minor * self.side + major

    def sign(self, ring):
        return 1 if ring % 2 == 0 else -1


def enter(torus, core, pos, extra=()):
    barrier = pltpu.get_barrier_semaphore()
    nexts = []
    for ring in range(RINGS):
        chip = torus.chip_at(ring, pos[ring] + torus.sign(ring))
        nexts.append(chip * CORES + core)
    for device in [*nexts, *extra]:
        pl.semaphore_signal(barrier, inc=1, device_id={"tp": device}, device_id_type=MESH_ID)
    pl.semaphore_wait(barrier, RINGS + len(extra))
    return nexts


def reduce_kernel(torus, ctx0, ctx1, up0, up1, wo0, wo1, wd0, wd1, res_ref, gain_ref, bias_ref, x_ref, n_ref,
                  h_buf, w_buf, part, acc, load_sem, send_sem, recv_sem):
    core, x, y = torus.me()
    pos = [torus.position(ring, x, y) for ring in range(RINGS)]
    heads, cols = ctx0.shape[2], up0.shape[2]
    d_model = w_buf.shape[1]
    quarter = d_model // RINGS
    rows = h_buf.shape[1]
    last = torus.chips - 1

    copies = []
    start = 0
    for i, (h_src, w_src, width) in enumerate(((ctx0, wo0, heads), (up0, wd0, cols), (ctx1, wo1, heads), (up1, wd1, cols))):
        copies.append(pltpu.make_async_copy(h_src, h_buf.at[:, :, pl.ds(start, width)], load_sem.at[2 * i]))
        copies.append(pltpu.make_async_copy(w_src, w_buf.at[pl.ds(start, width), :], load_sem.at[2 * i + 1]))
        start += width
    for copy in copies:
        copy.start()
    nexts = enter(torus, core, pos)
    for copy in copies:
        copy.wait()

    tile = min(512, quarter)

    def compute(step):
        for ring in range(RINGS):
            block = torus.chip_at(ring, pos[ring] - torus.sign(ring) * (1 + step))

            @pl.loop(0, quarter // tile)
            def _(j):
                off = pl.multiple_of(j * tile, tile)
                part[ring, :, pl.ds(off, tile)] = jnp.dot(
                    h_buf[block], w_buf[:, pl.ds(pl.multiple_of(ring * quarter + off, tile), tile)],
                    preferred_element_type=F32)

    def send(ring, step):
        return pltpu.make_async_remote_copy(
            src_ref=acc.at[ring, step], dst_ref=acc.at[ring, step + 1], send_sem=send_sem.at[ring],
            recv_sem=recv_sem.at[ring, step], device_id={"tp": nexts[ring]}, device_id_type=MESH_ID)

    compute(0)
    for ring in range(RINGS):
        acc[ring, 0] = part[ring].astype(BF16)
        send(ring, 0).start()

    @pl.loop(1, last)
    def _(step):
        compute(step)
        for ring in range(RINGS):
            send(ring, step - 1).wait_recv()
            acc[ring, step] = (acc[ring, step].astype(F32) + part[ring]).astype(BF16)
            send(ring, step).start()

    compute(last)
    for ring in range(RINGS):
        send(ring, last - 1).wait_recv()

    chunk = 16

    @pl.loop(0, rows // chunk)
    def _(i):
        rs = pl.ds(pl.multiple_of(i * chunk, chunk), chunk)
        total = jnp.concatenate([acc[ring, last, rs].astype(F32) + part[ring, rs] for ring in range(RINGS)], axis=1)
        new = (res_ref[rs].astype(F32) + total.astype(BF16).astype(F32)).astype(BF16)
        x_ref[rs] = new
        n_ref[rs] = layer_norm(new, gain_ref[...], bias_ref[...])

    for ring in range(RINGS):
        done = acc.at[ring, pl.ds(0, last)]
        pltpu.make_async_copy(done, done, send_sem.at[ring]).wait()


def reduce_layer(torus, ctxs, ups, w_outs, w_downs, residual, gain, bias):
    rows, d_model = residual.shape
    depth = sum(a.shape[2] for a in (*ctxs, *ups))
    quarter = d_model // RINGS
    anys = [pl.BlockSpec(memory_space=pl.ANY)] * 8
    vmem = pl.BlockSpec(memory_space=pltpu.VMEM)
    return pl.pallas_call(
        functools.partial(reduce_kernel, torus),
        name="reduce_layer",
        out_shape=[jax.ShapeDtypeStruct((rows, d_model), BF16)] * 2,
        in_specs=[*anys, vmem, vmem, vmem],
        out_specs=[vmem, vmem],
        scratch_shapes=[
            pltpu.VMEM((torus.chips, rows, depth), BF16),
            pltpu.VMEM((depth, d_model), BF16),
            pltpu.VMEM((RINGS, rows, quarter), F32),
            pltpu.VMEM((RINGS, torus.chips, rows, quarter), BF16),
            pltpu.SemaphoreType.DMA((8,)),
            pltpu.SemaphoreType.DMA((RINGS,)),
            pltpu.SemaphoreType.DMA((RINGS, torus.chips - 1)),
        ],
        compiler_params=pltpu.CompilerParams(collective_id=0, has_side_effects=True, vmem_limit_bytes=VMEM_LIMIT),
    )(*ctxs, *ups, *w_outs, *w_downs, residual, gain.reshape(1, -1), bias.reshape(1, -1))


def project_kernel(torus, n_ref, wq0, wu0, wq1, wu1, out_ref, w_buf, got, stage, load_sem, send_sem, recv_sem):
    core, x, y = torus.me()
    pos = [torus.position(ring, x, y) for ring in range(RINGS)]
    rows = n_ref.shape[0]
    share = rows // RINGS
    last = torus.chips - 1
    copies = []
    start = 0
    for i, w_src in enumerate((wq0, wu0, wq1, wu1)):
        width = w_src.shape[1]
        copies.append(pltpu.make_async_copy(w_src, w_buf.at[:, pl.ds(start, width)], load_sem.at[i]))
        start += width
    own_chip = y * torus.side + x
    own = pltpu.make_async_copy(n_ref, got.at[own_chip], load_sem.at[4])
    own.start()
    for copy in copies:
        copy.start()
    nexts = enter(torus, core, pos)
    own.wait()

    def block(ring, step):
        return torus.chip_at(ring, pos[ring] - torus.sign(ring) * step)

    def piece(ring, step):
        return got.at[block(ring, step), pl.ds(ring * share, share)]

    def send(ring, step):
        return pltpu.make_async_remote_copy(
            src_ref=piece(ring, step), dst_ref=piece(ring, step), send_sem=send_sem.at[ring],
            recv_sem=recv_sem.at[ring, step], device_id={"tp": nexts[ring]}, device_id_type=MESH_ID)

    def arrived(ring, step):
        return pltpu.make_async_remote_copy(
            src_ref=piece(ring, step + 1), dst_ref=piece(ring, step + 1), send_sem=send_sem.at[ring],
            recv_sem=recv_sem.at[ring, step], device_id={"tp": nexts[ring]}, device_id_type=MESH_ID)

    width = w_buf.shape[1]
    tile = 256

    def compute(step):
        for ring in range(RINGS):
            stage[pl.ds(ring * share, share)] = got[block(ring, step), pl.ds(ring * share, share)]

        @pl.loop(0, width // tile)
        def _(j):
            cs = pl.ds(pl.multiple_of(j * tile, tile), tile)
            res = jnp.dot(stage[...], w_buf[:, cs], preferred_element_type=F32)
            for ring in range(RINGS):
                rs = slice(ring * share, (ring + 1) * share)
                out_ref[block(ring, step), rs, cs] = res[rs]

    for ring in range(RINGS):
        send(ring, 0).start()
    for copy in copies:
        copy.wait()
    compute(0)

    @pl.loop(1, last)
    def _(step):
        for ring in range(RINGS):
            arrived(ring, step - 1).wait_recv()
            send(ring, step).start()
        compute(step)

    for ring in range(RINGS):
        arrived(ring, last - 1).wait_recv()
    compute(last)
    for ring in range(RINGS):
        done = got.at[pl.ds(0, last), pl.ds(ring * share, share)]
        pltpu.make_async_copy(done, done, send_sem.at[ring]).wait()


def gather_project(torus, normed, w_qkvs, w_ups):
    rows, d_model = normed.shape
    width = sum(w.shape[1] for w in (*w_qkvs, *w_ups))
    anys = [pl.BlockSpec(memory_space=pl.ANY)] * 5
    return pl.pallas_call(
        functools.partial(project_kernel, torus),
        name="gather_project",
        out_shape=jax.ShapeDtypeStruct((torus.chips, rows, width), F32),
        in_specs=anys,
        out_specs=pl.BlockSpec(memory_space=pltpu.VMEM),
        scratch_shapes=[
            pltpu.VMEM((d_model, width), BF16),
            pltpu.VMEM((torus.chips, rows, d_model), BF16),
            pltpu.VMEM((rows, d_model), BF16),
            pltpu.SemaphoreType.DMA((5,)),
            pltpu.SemaphoreType.DMA((RINGS,)),
            pltpu.SemaphoreType.DMA((RINGS, torus.chips - 1)),
        ],
        compiler_params=pltpu.CompilerParams(collective_id=1, has_side_effects=True, vmem_limit_bytes=VMEM_LIMIT),
    )(normed, w_qkvs[0], w_ups[0], w_qkvs[1], w_ups[1])


def gather_kernel(torus, y_ref, out_ref, got, load_sem, send_sem, recv_sem, pair_sem, store_sem):
    core, x, y = torus.me()
    pos = [torus.position(ring, x, y) for ring in range(RINGS)]
    rows = y_ref.shape[0]
    share = rows // RINGS
    last = torus.chips - 1
    own_chip = y * torus.side + x
    own = pltpu.make_async_copy(y_ref, got.at[own_chip], load_sem.at[0])
    own.start()
    partner = own_chip * CORES + (CORES - 1 - core)
    nexts = enter(torus, core, pos, (partner,))
    own.wait()

    def block(ring, step):
        return torus.chip_at(ring, pos[ring] - torus.sign(ring) * step)

    def piece(ring, step):
        return got.at[block(ring, step), pl.ds(ring * share, share)]

    def send(ring, step):
        return pltpu.make_async_remote_copy(
            src_ref=piece(ring, step), dst_ref=piece(ring, step), send_sem=send_sem.at[ring],
            recv_sem=recv_sem.at[ring, step], device_id={"tp": nexts[ring]}, device_id_type=MESH_ID)

    def arrived(ring, step):
        return pltpu.make_async_remote_copy(
            src_ref=piece(ring, step + 1), dst_ref=piece(ring, step + 1), send_sem=send_sem.at[ring],
            recv_sem=recv_sem.at[ring, step], device_id={"tp": nexts[ring]}, device_id_type=MESH_ID)

    def spread(ring, step):
        dst = out_ref.at[core * torus.chips + block(ring, step), pl.ds(ring * share, share)]
        pltpu.make_async_remote_copy(
            src_ref=piece(ring, step), dst_ref=dst, send_sem=pair_sem.at[0], recv_sem=pair_sem.at[1],
            device_id={"tp": partner}, device_id_type=MESH_ID).start()
        pltpu.make_async_copy(piece(ring, step), dst, store_sem.at[0]).start()

    for ring in range(RINGS):
        send(ring, 0).start()
    for ring in range(RINGS):
        spread(ring, 0)

    @pl.loop(1, last)
    def _(step):
        for ring in range(RINGS):
            arrived(ring, step - 1).wait_recv()
            send(ring, step).start()
        for ring in range(RINGS):
            spread(ring, step)

    for ring in range(RINGS):
        arrived(ring, last - 1).wait_recv()
        spread(ring, last)
    for ring in range(RINGS):
        done = got.at[pl.ds(0, last), pl.ds(ring * share, share)]
        pltpu.make_async_copy(done, done, send_sem.at[ring]).wait()
    pltpu.make_async_copy(got, got, pair_sem.at[0]).wait()
    pltpu.make_async_copy(got, got, store_sem.at[0]).wait()
    pltpu.make_async_copy(got, got, pair_sem.at[1]).wait()


def gather_all(torus, y_own):
    rows, d_model = y_own.shape
    return pl.pallas_call(
        functools.partial(gather_kernel, torus),
        name="gather_all",
        out_shape=jax.ShapeDtypeStruct((CORES * torus.chips, rows, d_model), BF16),
        in_specs=[pl.BlockSpec(memory_space=pl.ANY)],
        out_specs=pl.BlockSpec(memory_space=pl.ANY),
        scratch_shapes=[
            pltpu.VMEM((torus.chips, rows, d_model), BF16),
            pltpu.SemaphoreType.DMA((1,)),
            pltpu.SemaphoreType.DMA((RINGS,)),
            pltpu.SemaphoreType.DMA((RINGS, torus.chips - 1)),
            pltpu.SemaphoreType.DMA((2,)),
            pltpu.SemaphoreType.DMA((1,)),
        ],
        compiler_params=pltpu.CompilerParams(collective_id=2, has_side_effects=True, vmem_limit_bytes=VMEM_LIMIT),
    )(y_own)


def solution(mesh):
    n_tp = mesh.shape["tp"]
    torus = Torus(math.isqrt(n_tp // CORES))
    swap = [(i, i ^ 1) for i in range(n_tp)]

    def shard_body(act_in, ln_gain, ln_bias, w_qkv, w_out, w_up, w_down):
        layers = ln_gain.shape[0]
        head_dim = w_out.shape[1]
        idx = lax.axis_index("tp")
        core, chip = lax.rem(idx, CORES), lax.div(idx, CORES)
        w_qkv = w_qkv[:, :, 0]
        mine = [[w[layer] for layer in range(layers)] for w in (w_qkv, w_up, w_out, w_down)]
        theirs = [[lax.ppermute(w[layer], "tp", swap) for layer in range(layers)] for w in mine]
        w_qkvs, w_ups, w_outs, w_downs = [list(zip(a, b)) for a, b in zip(mine, theirs)]

        half = lax.dynamic_slice_in_dim(act_in, core * torus.chips, torus.chips, 0)
        own = lax.dynamic_index_in_dim(half, chip, 0, keepdims=False)
        normed = layer_norm(half, ln_gain[0], ln_bias[0])
        for layer in range(layers):
            if layer == 0:
                qkvs = [jnp.einsum("bsd,dc->bsc", normed, w, preferred_element_type=F32) for w in w_qkvs[0]]
                raws = [jnp.einsum("bsd,dc->bsc", normed, w, preferred_element_type=F32) for w in w_ups[0]]
            else:
                proj = gather_project(torus, normed, w_qkvs[layer], w_ups[layer])
                nq, nu = w_qkvs[layer][0].shape[1], w_ups[layer][0].shape[1]
                qkvs = [proj[..., i * (nq + nu):i * (nq + nu) + nq] for i in range(CORES)]
                raws = [proj[..., i * (nq + nu) + nq:(i + 1) * (nq + nu)] for i in range(CORES)]
            ctxs = [attend(qkv, head_dim) for qkv in qkvs]
            ups = [jax.nn.gelu(raw, approximate=False).astype(BF16) for raw in raws]
            nxt = (layer + 1) % layers
            own, normed = reduce_layer(torus, ctxs, ups, w_outs[layer], w_downs[layer], own, ln_gain[nxt], ln_bias[nxt])
        return gather_all(torus, own)

    return jax.shard_map(shard_body, mesh=mesh, in_specs=(P("dp", None, None), P(None, None), P(None, None), P(None, None, "tp", None), P(None, "tp", None), P(None, None, "tp"), P(None, "tp", None)), out_specs=P("dp", None, None), check_vma=False)
```

time: 875 us -> 688 us (0.79)
  waiting for transfers between devices: 498 us -> 0.02 us
  Pallas kernels: 0 us -> 478 us
  matrix products: 235 us -> 93.9 us
  other arithmetic: 106 us -> 55.5 us
  local copies, waits for them, and re-layouts: 16.3 us -> 46.5 us
  between operations: 14.1 us -> 0.8 us
    psum x2 -> x0, waiting for transfers between devices: 498 us -> none  [shard_body(): reduced = lax.psum(local_sum, 'tp')]
    pallas_call x0 -> x4, Pallas kernels: none -> 478 us  [the longest x2 226 us: reduce_layer(): pl.pallas_call(functools.partial(reduce_kernel, torus), name='reduce_laye...]
    dot_general x10 -> x8, matrix products: 235 us -> 84.3 us  [the longest x4 72.3 us: shard_body(): jnp.einsum('bsd,dc->bsc', normed, w, preferred_element_type=F32)]
    reduce_sum x2 -> x1, other arithmetic: 44.5 us -> 6.85 us  [layer_norm(): row_mean = jnp.mean(hidden_f, axis=-1, keepdims=True)]
    squeeze x2 -> x5, local copies, waits for them, and re-layouts: 0.35 us -> 22.2 us  [the longest x4 19.8 us: shard_body(): w[layer]]
    another operation x0 -> x3, other arithmetic: none -> 18.8 us
    reduce_sum x2 -> x1, other arithmetic: 26 us -> 7.88 us  [layer_norm(): row_var = jnp.mean(centered * centered, axis=-1, keepdims=True)]
    unnamed x42 -> x53, local copies, waits for them, and re-layouts: 6.45 us -> 23.6 us
  transfers between devices with their start and end apart: 2 -> 8, of which waited for: 2 -> 0; matrix products, arithmetic and copies ran while one was open for 0% -> 25% of each run, Pallas kernels for 0% -> 33%
where the time goes in v1:
time: 688 us; the launch traced here: 679 us
  Pallas kernels  478 us (69%)
  matrix products  93.9 us (14%)
  other arithmetic  55.5 us (8%)
  local copies, waits for them, and re-layouts  46.5 us (7%)
    pallas_call x2, Pallas kernels, reduce_layer(): pl.pallas_call(functools.partial(reduce_kernel, torus), name='reduce_laye...  226 us
    pallas_call x1, Pallas kernels, gather_all(): pl.pallas_call(functools.partial(gather_kernel, torus), name='gather_all'...  142 us
    pallas_call x1, Pallas kernels, gather_project(): pl.pallas_call(functools.partial(project_kernel, torus), name='gather_pro...  110 us
    dot_general x4, matrix products, shard_body(): jnp.einsum('bsd,dc->bsc', normed, w, preferred_element_type=F32)  72.3 us
    unnamed x53, local copies, waits for them, and re-layouts  23.6 us
    convert_element_type x1, other arithmetic, shard_body(): ups = [jax.nn.gelu(raw, approximate=False).astype(BF16) for raw in raws]  20.4 us
    squeeze x4, local copies, waits for them, and re-layouts, shard_body(): w[layer]  19.8 us
    another operation x3, other arithmetic  18.8 us
  transfers between devices with their start and end apart: 8, of which 0 were waited for; matrix products, arithmetic and copies ran while one was open for 25% of the time, Pallas kernels for 33%

profile of v1, /device:TPU:97, one launch (start us, length us, event | category | flops | bytes accessed | tf_op | source)
XLA Modules:
  0.0 678.6 jit_solution(13386403232762614641)
XLA Ops:
  0.0 3.2 slice_bitcast_fusion.6
  3.2 2.0 collective-permute-start.6
  5.3 6.2 slice_bitcast_fusion.4
  12.1 3.5 slice_bitcast_fusion
  16.2 0.6 iota_compare_fusion
  16.8 6.9 %convert_reduce_fusion = f32[16,128]{1,0:T(8,128)S(1)} fusion(bf16[32,128,4096]{2,1,0:T(8,128)(2,1)} %param.7, s32[]{:T(128)S(6)} %select_n.24), kind=kLoop, calls=%fused_computation.5 | loop fusion | flops 16775168 | bytes 16785412 | tf_op jit(solution)/shard_map/reduce_sum | solution.py:23
  23.6 7.9 %fusion.6 = f32[16,128]{1,0:T(8,128)S(1)} fusion(f32[16,128]{1,0:T(8,128)S(1)} %broadcast_multiply_fusion, bf16[32,128,4096]{2,1,0:T(8,128)(2,1)} %param.7, s32[]{:T(128)S(6)} %select_n.24), kind=kLoop, calls=%fused_computation.8 | loop fusion | flops 33552384 | bytes 16793604 | tf_op jit(solution)/shard_map/reduce_sum | solution.py:25
  31.5 0.9 fusion.119
  32.5 2.4 dynamic-slice_bitcast_fusion.res_ref
  34.9 6.8 %slice_bitcast_fusion.1 = (bf16[4096,512]{1,0:T(8,128)(2,1)}, bf16[4096,512]{1,0:T(8,128)(2,1)}) fusion(bf16[2,4096,512]{2,1,0:T(8,128)(2,1)} %param.12), kind=kLoop, calls=%fused_computation.59 | loop fusion | bytes 16777216 | tf_op jit(solution)/shard_map/squeeze | solution.py:375
  41.7 0.7 fusion.204
  43.0 22.2 %fusion.12.up0 = bf16[16,128,512]{2,1,0:T(8,128)(2,1)} fusion(bf16[2,4096,512]{2,1,0:T(8,128)(2,1)S(1)} %bitcast.40, f32[4096]{0:T(1024)S(1)} %bitcast.43, f32[4096]{0:T(1024)S(1)} %bitcast.47, f32[16,128]{1,0:T(8,128)S(1)} %add_rsqrt_fusion, f32[16,128]{1,0:T(8,128)S(1)} %broadcast_multiply_fusion, bf16[32,128,4096]{2,1,0:T(8,128)(2,1)} %param.7, ...), kind=kOutput, calls=%fused_computation.18 | convolution fusion | flops 8708423680 | bytes 23117828 | tf_op jit(solution)/shard_map/bsd,dc->bsc/dot_general | solution.py:385
  65.3 14.8 %fusion.55 = f32[16,128,384]{2,1,0:T(8,128)S(1)} fusion(bf16[2,4096,1,384]{3,1,2,0:T(8,128)(2,1)S(1)} %bitcast.42, f32[4096]{0:T(1024)} %bitcast.44, f32[4096]{0:T(1024)} %bitcast.48, f32[16,128]{1,0:T(8,128)} %copy-done.16, f32[16,128]{1,0:T(8,128)S(1)} %broadcast_multiply_fusion, bf16[32,128,4096]{2,1,0:T(8,128)(2,1)} %param.7, s32[]{:T(128)S(6)} %select_n.24), kind=kOutput, calls=%fused_computation.97 | convolution fusion | flops 6492782592 | bytes 23117828 | tf_op jit(solution)/shard_map/bsd,dc->bsc/dot_general | solution.py:384
  80.3 13.0 %fusion.57 = f32[16,128,384]{2,1,0:T(8,128)S(1)} fusion(bf16[4096,384]{1,0:T(8,128)(2,1)} %collective-permute-done, f32[4096]{0:T(1024)S(1)} %bitcast.45, f32[4096]{0:T(1024)S(1)} %bitcast.49, f32[16,128]{1,0:T(8,128)S(1)} %copy-done.17, f32[16,128]{1,0:T(8,128)S(1)} %broadcast_multiply_fusion, bf16[32,128,4096]{2,1,0:T(8,128)(2,1)} %param.7, s32[]{:T(128)S(6)} %select_n.24), kind=kOutput, calls=%fused_computation.99 | convolution fusion | flops 6492782592 | bytes 23117828 | tf_op jit(solution)/shard_map/bsd,dc->bsc/dot_general | solution.py:384
  93.4 3.5 subtract_convert_fusion.4
  96.8 2.4 fusion.211
  99.2 2.4 fusion.206
  101.6 3.7 convolution_convert_fusion.2.ctx1
  105.3 3.4 convolution_convert_fusion.3.ctx0
  109.2 22.2 %fusion.15.up1 = bf16[16,128,512]{2,1,0:T(8,128)(2,1)} fusion(bf16[4096,512]{1,0:T(8,128)(2,1)} %collective-permute-done.1, f32[4096]{0:T(1024)S(1)} %bitcast.46, f32[4096]{0:T(1024)S(1)} %bitcast.50, f32[16,128]{1,0:T(8,128)S(1)} %copy-done.18, f32[16,128]{1,0:T(8,128)S(1)} %broadcast_multiply_fusion, bf16[32,128,4096]{2,1,0:T(8,128)(2,1)} %param.7, ...), kind=kOutput, calls=%fused_computation.21 | convolution fusion | flops 8708423680 | bytes 23117828 | tf_op jit(solution)/shard_map/bsd,dc->bsc/dot_general | solution.py:385
  131.5 115.7 %reduce_layer.2 = (bf16[128,4096]{1,0:T(8,128)(2,1)}, bf16[128,4096]{1,0:T(8,128)(2,1)}) custom-call(bf16[16,128,128]{2,1,0:T(8,128)(2,1)} %convolution_convert_fusion.3.ctx0, bf16[16,128,128]{2,1,0:T(8,128)(2,1)} %convolution_convert_fusion.2.ctx1, bf16[16,128,512]{2,1,0:T(8,128)(2,1)} %fusion.12.up0, bf16[16,128,512]{2,1,0:T(8,128)(2,1)} %fusion.15.up1, ...), custom_call_target="tpu_custom_call" | custom-call | tf_op jit(solution)/shard_map/reduce_layer/pallas_call | solution.py:171
  247.3 110.1 %gather_project.1 = f32[16,128,1792]{2,1,0:T(8,128)} custom-call(bf16[128,4096]{1,0:T(8,128)(2,1)} %get-tuple-element.8.n_ref, bf16[4096,384]{1,0:T(8,128)(2,1)} %get-tuple-element.25.wq0, bf16[4096,512]{1,0:T(8,128)(2,1)} %get-tuple-element.23.wu0, bf16[4096,384]{1,0:T(8,128)(2,1)} %collective-permute-done.4.wq1, bf16[4096,512]{1,0:T(8,128)(2,1)} %collective-permute-done.5.wu1), custom_call_target="tpu_custom_call" | custom-call | tf_op jit(solution)/shard_map/gather_project/pallas_call | solution.py:266
  357.4 6.2 subtract_convert_fusion
  363.6 9.1 %convert.72 = bf16[16,128,1792]{2,1,0:T(8,128)(2,1)} convert(f32[16,128,1792]{2,1,0:T(8,128)} %gather_project.1) | non-fusion elementwise | flops 3670016 | bytes 22020096 | tf_op jit(solution)/shard_map/convert.5
  372.7 20.4 %fusion.21 = (bf16[16,128,512]{2,1,0:T(8,128)(2,1)}, bf16[16,128,512]{2,1,0:T(8,128)(2,1)}) fusion(f32[16,128,1792]{2,1,0:T(8,128)} %gather_project.1), kind=kLoop, calls=%fused_computation.27 | loop fusion | flops 136314880 | bytes 12582912 | tf_op jit(solution)/shard_map/convert_element_type | solution.py:392
  393.1 3.0 fusion.221
  396.2 1.9 fusion.216
  398.0 2.6 convolution_convert_fusion.ctx1
  400.6 2.2 convolution_convert_fusion.1.ctx0
  402.9 109.9 %reduce_layer.3 = (bf16[128,4096]{1,0:T(8,128)(2,1)}, bf16[128,4096]{1,0:T(8,128)(2,1)}) custom-call(bf16[16,128,128]{2,1,0:T(8,128)(2,1)} %convolution_convert_fusion.1.ctx0, bf16[16,128,128]{2,1,0:T(8,128)(2,1)} %convolution_convert_fusion.ctx1, bf16[16,128,512]{2,1,0:T(8,128)(2,1)} %get-tuple-element.20.up0, bf16[16,128,512]{2,1,0:T(8,128)(2,1)} %get-tuple-element.19.up1, ...), custom_call_target="tpu_custom_call" | custom-call | tf_op jit(solution)/shard_map/reduce_layer/pallas_call | solution.py:171
  512.7 142.5 %gather_all.1 = bf16[32,128,4096]{2,1,0:T(8,128)(2,1)} custom-call(bf16[128,4096]{1,0:T(8,128)(2,1)} %get-tuple-element.10.y_ref), custom_call_target="tpu_custom_call" | custom-call | tf_op jit(solution)/shard_map/gather_all/pallas_call | solution.py:346
  655.2 22.9 %copy.17 = bf16[32,128,4096]{2,1,0:T(8,128)(2,1)} copy(bf16[32,128,4096]{2,1,0:T(8,128)(2,1)} %gather_all.1) | data formatting | bytes 67108864
  (73 shorter events, 2.5 us)
Async XLA Ops:
  0.0 12.1 %slice-start = ((s8[8388608]{0:T(1024)(128)(4,1)}), s8[4194304]{0:T(1024)(128)(4,1)S(1)}, s32[]{:S(2)}) async-start(s8[8388608]{0:T(1024)(128)(4,1)} %bitcast.37), calls=%async_computation | async-start | bytes 8388608
  3.2 399.6 %collective-permute-start.6 = (bf16[128,4096]{1,0:T(8,128)(2,1)}, bf16[128,4096]{1,0:T(8,128)(2,1)}, u32[]{:S(2)}, u32[]{:S(2)}) collective-permute-start(bf16[128,4096]{1,0:T(8,128)(2,1)} %get-tuple-element.35.wo0), channel_id=1, source_target_pairs={{0,1},{1,0},{2,3},{3,2},{4,5},{5,4},{6,7},{7,6},{8,9},{9,8},{10,11... | collective-permute-start | bytes 3145736 | tf_op jit(solution)/shard_map/ppermute | solution.py:376
  5.3 6.9 %slice-start.1 = ((s8[8388608]{0:T(1024)(128)(4,1)}), s8[4194304]{0:T(1024)(128)(4,1)S(1)}, s32[]{:S(2)}) async-start(s8[8388608]{0:T(1024)(128)(4,1)} %bitcast.37), calls=%async_computation.1 | async-start | bytes 8388608
  5.3 126.2 %collective-permute-start.2 = (bf16[128,4096]{1,0:T(8,128)(2,1)}, bf16[128,4096]{1,0:T(8,128)(2,1)}, u32[]{:S(2)}, u32[]{:S(2)}) collective-permute-start(bf16[128,4096]{1,0:T(8,128)(2,1)} %get-tuple-element.36.wo0), channel_id=1, source_target_pairs={{0,1},{1,0},{2,3},{3,2},{4,5},{5,4},{6,7},{7,6},{8,9},{9,8},{10,11... | collective-permute-start | bytes 3145736 | tf_op jit(solution)/shard_map/ppermute | solution.py:376
  11.5 68.6 %collective-permute-start = (bf16[4096,384]{1,0:T(8,128)(2,1)}, bf16[4096,384]{1,0:T(8,128)(2,1)}, u32[]{:S(2)}, u32[]{:S(2)}) collective-permute-start(bf16[4096,384]{1,0:T(8,128)(2,1)} %get-tuple-element.26), channel_id=1, source_target_pairs={{0,1},{1,0},{2,3},{3,2},{4,5},{5,4},{6,7},{7,6},{8,9},{9,8},{10,11... | collective-permute-start | bytes 9437192 | tf_op jit(solution)/shard_map/ppermute | solution.py:376
  12.1 235.1 %collective-permute-start.4 = (bf16[4096,384]{1,0:T(8,128)(2,1)}, bf16[4096,384]{1,0:T(8,128)(2,1)}, u32[]{:S(2)}, u32[]{:S(2)}) collective-permute-start(bf16[4096,384]{1,0:T(8,128)(2,1)} %get-tuple-element.25.wq0), channel_id=1, source_target_pairs={{0,1},{1,0},{2,3},{3,2},{4,5},{5,4},{6,7},{7,6},{8,9},{9,8},{10,11... | collective-permute-start | bytes 9437192 | tf_op jit(solution)/shard_map/ppermute | solution.py:376
  15.7 115.9 %collective-permute-start.3 = (bf16[512,4096]{1,0:T(8,128)(2,1)}, bf16[512,4096]{1,0:T(8,128)(2,1)}, u32[]{:S(2)}, u32[]{:S(2)}) collective-permute-start(bf16[512,4096]{1,0:T(8,128)(2,1)} %get-tuple-element.22.wd0), channel_id=1, source_target_pairs={{0,1},{1,0},{2,3},{3,2},{4,5},{5,4},{6,7},{7,6},{8,9},{9,8},{10,11... | collective-permute-start | bytes 12582920 | tf_op jit(solution)/shard_map/ppermute | solution.py:376
  31.5 10.8 %copy-start.16 = (f32[16,128]{1,0:T(8,128)}, f32[16,128]{1,0:T(8,128)S(1)}, u32[]{:S(2)}) copy-start(f32[16,128]{1,0:T(8,128)S(1)} %add_rsqrt_fusion) | copy-start | bytes 24580
  32.5 10.5 %slice-start.2 = ((s8[8388608]{0:T(1024)(128)(4,1)}), s8[4194304]{0:T(1024)(128)(4,1)S(1)}, s32[]{:S(2)}) async-start(s8[8388608]{0:T(1024)(128)(4,1)} %bitcast.39), calls=%async_computation.2 | async-start | bytes 8388608
  34.9 6.8 %copy-start.12 = (f32[2,4096]{1,0:T(2,128)S(1)}, f32[2,4096]{1,0:T(2,128)}, u32[]{:S(2)}) copy-start(f32[2,4096]{1,0:T(2,128)} %param.9) | copy-start | bytes 98308
  34.9 6.8 %copy-start.13 = (f32[2,4096]{1,0:T(2,128)S(1)}, f32[2,4096]{1,0:T(2,128)}, u32[]{:S(2)}) copy-start(f32[2,4096]{1,0:T(2,128)} %param.8) | copy-start | bytes 98308
  34.9 8.1 %slice-start.3 = ((s8[8388608]{0:T(1024)(128)(4,1)}), s8[4194304]{0:T(1024)(128)(4,1)S(1)}, s32[]{:S(2)}) async-start(s8[8388608]{0:T(1024)(128)(4,1)} %bitcast.39), calls=%async_computation.3 | async-start | bytes 8388608
  34.9 30.3 %slice-start.4 = ((s8[6291456]{0:T(1024)(128)(4,1)}), s8[4194304]{0:T(1024)(128)(4,1)S(1)}, s32[]{:S(2)}) async-start(s8[6291456]{0:T(1024)(128)(4,1)} %bitcast.41), calls=%async_computation.4 | async-start | bytes 8388608
  43.0 22.3 %slice-start.5 = ((s8[6291456]{0:T(1024)(128)(4,1)}), s8[2097152]{0:T(1024)(128)(4,1)S(1)}, s32[]{:S(2)}) async-start(s8[6291456]{0:T(1024)(128)(4,1)} %bitcast.41), calls=%async_computation.5 | async-start | bytes 4194304
  65.2 15.0 %copy-start.7 = (f32[1,4096]{1,0:T(1,128)S(1)}, f32[1,4096]{1,0:T(1,128)}, u32[]{:S(2)}) copy-start(f32[1,4096]{1,0:T(1,128)} %copy-done.6) | copy-start | bytes 49156
  65.3 15.0 %copy-start.10 = (f32[1,4096]{1,0:T(1,128)S(1)}, f32[1,4096]{1,0:T(1,128)}, u32[]{:S(2)}) copy-start(f32[1,4096]{1,0:T(1,128)} %copy-done.9) | copy-start | bytes 49156
  65.3 15.0 %copy-start.17 = (f32[16,128]{1,0:T(8,128)S(1)}, f32[16,128]{1,0:T(8,128)}, u32[]{:S(2)}) copy-start(f32[16,128]{1,0:T(8,128)} %copy-done.16) | copy-start | bytes 24580
  80.1 13.2 %copy-start.1 = (f32[128,64]{1,0:T(8,128)S(1)}, f32[128,64]{1,0:T(8,128)}, u32[]{:S(2)}) copy-start(f32[128,64]{1,0:T(8,128)} %get-tuple-element.45) | copy-start | bytes 98308
  80.1 13.2 %copy-start.3 = (f32[128,64]{1,0:T(8,128)S(1)}, f32[128,64]{1,0:T(8,128)}, u32[]{:S(2)}) copy-start(f32[128,64]{1,0:T(8,128)} %get-tuple-element.46) | copy-start | bytes 98308
  80.1 28.6 %collective-permute-start.1 = (bf16[4096,512]{1,0:T(8,128)(2,1)}, bf16[4096,512]{1,0:T(8,128)(2,1)}, u32[]{:S(2)}, u32[]{:S(2)}) collective-permute-start(bf16[4096,512]{1,0:T(8,128)(2,1)} %get-tuple-element.24), channel_id=1, source_target_pairs={{0,1},{1,0},{2,3},{3,2},{4,5},{5,4},{6,7},{7,6},{8,9},{9,8},{10,11... | collective-permute-start | bytes 12582920 | tf_op jit(solution)/shard_map/ppermute | solution.py:376
  93.3 3.5 copy-start
  93.4 3.5 copy-start.14
  105.3 3.9 copy-start.8
  105.3 3.9 copy-start.11
  105.3 3.9 copy-start.18
  108.8 138.5 %collective-permute-start.5 = (bf16[4096,512]{1,0:T(8,128)(2,1)}, bf16[4096,512]{1,0:T(8,128)(2,1)}, u32[]{:S(2)}, u32[]{:S(2)}) collective-permute-start(bf16[4096,512]{1,0:T(8,128)(2,1)} %get-tuple-element.23.wu0), channel_id=1, source_target_pairs={{0,1},{1,0},{2,3},{3,2},{4,5},{5,4},{6,7},{7,6},{8,9},{9,8},{10,11... | collective-permute-start | bytes 12582920 | tf_op jit(solution)/shard_map/ppermute | solution.py:376
  131.5 271.4 %collective-permute-start.7 = (bf16[512,4096]{1,0:T(8,128)(2,1)}, bf16[512,4096]{1,0:T(8,128)(2,1)}, u32[]{:S(2)}, u32[]{:S(2)}) collective-permute-start(bf16[512,4096]{1,0:T(8,128)(2,1)} %get-tuple-element.21.wd0), channel_id=1, source_target_pairs={{0,1},{1,0},{2,3},{3,2},{4,5},{5,4},{6,7},{7,6},{8,9},{9,8},{10,11... | collective-permute-start | bytes 12582920 | tf_op jit(solution)/shard_map/ppermute | solution.py:376
  247.2 110.2 %copy-start.2 = (f32[128,64]{1,0:T(8,128)S(1)}, f32[128,64]{1,0:T(8,128)}, u32[]{:S(2)}) copy-start(f32[128,64]{1,0:T(8,128)} %get-tuple-element.45) | copy-start | bytes 98308
  247.2 110.2 %copy-start.4 = (f32[128,64]{1,0:T(8,128)S(1)}, f32[128,64]{1,0:T(8,128)}, u32[]{:S(2)}) copy-start(f32[128,64]{1,0:T(8,128)} %get-tuple-element.46) | copy-start | bytes 98308
  372.7 20.4 %copy-start.5 = (bf16[16,128,64]{2,1,0:T(8,128)(2,1)S(1)}, bf16[16,128,64]{2,1,0:T(8,128)(2,1)}, u32[]{:S(2)}) copy-start(bf16[16,128,64]{2,1,0:T(8,128)(2,1)} %get-tuple-element.12) | copy-start | bytes 786436
  372.7 20.4 %copy-start.15 = (pred[128,128]{0,1:T(8,128)(4,1)S(1)}, pred[128,128]{0,1:T(8,128)(4,1)}, u32[]{:S(2)}) copy-start(pred[128,128]{0,1:T(8,128)(4,1)} %iota_compare_fusion) | copy-start | bytes 49156
  398.0 2.6 copy-start.19
  (2 other events, 1.2 us)

commit v2 on v1

v2 whole, which is shorter than its diff:
```python
import functools
import math

import jax
import jax.numpy as jnp
from jax import lax
from jax.experimental import pallas as pl
from jax.experimental.pallas import tpu as pltpu
from jax.sharding import PartitionSpec as P

LN_EPS = 1e-5
ROPE_BASE = 10000.0
CORES = 2
RINGS = 4
SUBS = 2
MESH_ID = pl.DeviceIdType.MESH
BF16 = jnp.bfloat16
F32 = jnp.float32
VMEM_LIMIT = 66_000_000


def layer_norm(hidden, gain, bias):
    hidden_f = hidden.astype(F32)
    row_mean = jnp.mean(hidden_f, axis=-1, keepdims=True)
    centered = hidden_f - row_mean
    row_var = jnp.mean(centered * centered, axis=-1, keepdims=True)
    return (centered * lax.rsqrt(row_var + LN_EPS) * gain + bias).astype(BF16)


def rope_tables(seq_len, head_dim):
    half_dim = head_dim // 2
    inv_freq = ROPE_BASE ** (-2.0 * jnp.arange(half_dim, dtype=F32) / head_dim)
    angles = jnp.arange(seq_len, dtype=F32)[:, None] * inv_freq[None, :]
    return jnp.cos(angles), jnp.sin(angles)


def apply_rope(proj, cos_tab, sin_tab):
    half_dim = proj.shape[-1] // 2
    first = proj[..., :half_dim]
    second = proj[..., half_dim:]
    return jnp.concatenate([first * cos_tab - second * sin_tab, second * cos_tab + first * sin_tab], axis=-1)


def attend(qkv, head_dim):
    seq_len = qkv.shape[1]
    cos_tab, sin_tab = rope_tables(seq_len, head_dim)
    query = apply_rope(qkv[..., :head_dim], cos_tab, sin_tab).astype(BF16)
    keys = apply_rope(qkv[..., head_dim:2 * head_dim], cos_tab, sin_tab).astype(BF16)
    values = qkv[..., 2 * head_dim:].astype(BF16)
    scores = jnp.einsum("bsd,btd->bst", query, keys, preferred_element_type=F32) * (head_dim ** -0.5)
    positions = jnp.arange(seq_len)
    scores = jnp.where(positions[:, None] >= positions[None, :], scores, -1e30)
    probs = jax.nn.softmax(scores, axis=-1).astype(BF16)
    return jnp.einsum("bst,btd->bsd", probs, values, preferred_element_type=F32).astype(BF16)


class Torus:
    def __init__(self, side):
        self.side = side
        self.chips = side * side

    def me(self):
        idx = lax.axis_index("tp")
        core = lax.rem(idx, CORES)
        chip = lax.div(idx, CORES)
        return core, lax.rem(chip, self.side), lax.div(chip, self.side)

    def position(self, ring, x, y):
        major = y if ring < 2 else x
        return self.side * major + lax.rem(x + y, self.side)

    def chip_at(self, ring, pos):
        pos = lax.rem(pos + 2 * self.chips, self.chips)
        major = lax.div(pos, self.side)
        minor = lax.rem(lax.rem(pos, self.side) - major + self.side, self.side)
        return major * self.side + minor if ring < 2 else minor * self.side + major

    def sign(self, ring):
        return 1 if ring % 2 == 0 else -1


def enter(torus, core, pos, extra=()):
    barrier = pltpu.get_barrier_semaphore()
    nexts = []
    for ring in range(RINGS):
        chip = torus.chip_at(ring, pos[ring] + torus.sign(ring))
        nexts.append(chip * CORES + core)
    for device in [*nexts, *extra]:
        pl.semaphore_signal(barrier, inc=1, device_id={"tp": device}, device_id_type=MESH_ID)
    pl.semaphore_wait(barrier, RINGS + len(extra))
    return nexts


def gelu(x):
    return 0.5 * x * (1.0 + lax.erf(x * (0.5 ** 0.5)))


def reduce_kernel(torus, layer, from_normed, last_layer, *refs):
    (src_ref, ctx0, ctx1, wo0, wo1, wd0, wd1, wu0, wu1, res_ref, gain_ref, bias_ref), refs = refs[:12], refs[12:]
    if last_layer:
        x_ref, n_ref, refs = refs[0], None, refs[1:]
    else:
        x_ref, n_ref, refs = refs[0], refs[1], refs[2:]
    ctx_buf, w_buf, up_buf, rows_buf, stage, part, acc, load_sem, row_sem, send_sem, recv_sem = refs
    core, x, y = torus.me()
    pos = [torus.position(ring, x, y) for ring in range(RINGS)]
    heads, cols = ctx0.shape[2], wd0.shape[1]
    d_model = w_buf.shape[1]
    rows = stage.shape[0]
    share = rows // RINGS
    last = torus.chips - 1
    ctx_width = CORES * heads

    def block(ring, step):
        return torus.chip_at(ring, pos[ring] - torus.sign(ring) * (1 + step))

    def fetch(ring, step, slot):
        return pltpu.make_async_copy(
            src_ref.at[block(ring, step), pl.ds(ring * share, share)],
            rows_buf.at[slot, pl.ds(ring * share, share)], row_sem.at[slot, ring])

    for ring in range(RINGS):
        fetch(ring, 0, 0).start()
    copies = []
    if from_normed:
        for i, w_src in enumerate((wu0, wu1)):
            copies.append(pltpu.make_async_copy(w_src.at[layer], up_buf.at[:, pl.ds(i * cols, cols)], load_sem.at[i]))
    for i, src in enumerate((ctx0, ctx1)):
        copies.append(pltpu.make_async_copy(src, ctx_buf.at[:, :, pl.ds(i * heads, heads)], load_sem.at[2 + i]))
    start = 0
    for i, (w_src, width) in enumerate(((wo0, heads), (wo1, heads), (wd0, cols), (wd1, cols))):
        copies.append(pltpu.make_async_copy(w_src.at[layer], w_buf.at[pl.ds(start, width), :], load_sem.at[4 + i]))
        start += width
    for copy in copies:
        copy.start()
    nexts = enter(torus, core, pos)
    for copy in copies:
        copy.wait()

    tile = 256
    wide = 512

    def compute(step, slot, more):
        if more:
            for ring in range(RINGS):
                fetch(ring, step + 1, 1 - slot).start()
        for ring in range(RINGS):
            stage[pl.ds(ring * share, share), 0:ctx_width] = ctx_buf[block(ring, step), pl.ds(ring * share, share)]
            fetch(ring, step, slot).wait()
        if from_normed:
            @pl.loop(0, CORES * cols // tile)
            def _(j):
                cs = pl.multiple_of(j * tile, tile)
                raw = jnp.dot(rows_buf[slot], up_buf[:, pl.ds(cs, tile)], preferred_element_type=F32)
                stage[:, pl.ds(pl.multiple_of(ctx_width + cs, 128), tile)] = gelu(raw).astype(BF16)
        else:
            stage[:, ctx_width:] = rows_buf[slot]

    narrow = d_model // SUBS

    def down(sub):
        @pl.loop(0, narrow // wide)
        def _(j):
            cs = pl.ds(pl.multiple_of(sub * narrow + j * wide, wide), wide)
            part[:, cs] = jnp.dot(stage[...], w_buf[:, cs], preferred_element_type=F32)

    def mine(ring, sub):
        return part[pl.ds(ring * share, share), sub * narrow:(sub + 1) * narrow]

    def send(ring, sub, step):
        return pltpu.make_async_remote_copy(
            src_ref=acc.at[ring, sub, step], dst_ref=acc.at[ring, sub, step + 1], send_sem=send_sem.at[ring, sub],
            recv_sem=recv_sem.at[ring, sub, step], device_id={"tp": nexts[ring]}, device_id_type=MESH_ID)

    compute(0, 0, True)
    for sub in range(SUBS):
        down(sub)
        for ring in range(RINGS):
            acc[ring, sub, 0] = mine(ring, sub).astype(BF16)
            send(ring, sub, 0).start()

    @pl.loop(1, last)
    def _(step):
        compute(step, lax.rem(step, 2), True)
        for sub in range(SUBS):
            down(sub)
            for ring in range(RINGS):
                send(ring, sub, step - 1).wait_recv()
                acc[ring, sub, step] = (acc[ring, sub, step].astype(F32) + mine(ring, sub)).astype(BF16)
                send(ring, sub, step).start()

    compute(last, last % 2, False)
    for sub in range(SUBS):
        down(sub)
        for ring in range(RINGS):
            send(ring, sub, last - 1).wait_recv()

    chunk = 16
    per = share // chunk

    @pl.loop(0, rows // chunk)
    def _(i):
        rs = pl.ds(pl.multiple_of(i * chunk, chunk), chunk)
        sub = pl.ds(pl.multiple_of(lax.rem(i, per) * chunk, chunk), chunk)
        total = jnp.concatenate([acc[lax.div(i, per), half, last, sub] for half in range(SUBS)], axis=1).astype(F32) + part[rs]
        new = (res_ref[rs].astype(F32) + total.astype(BF16).astype(F32)).astype(BF16)
        x_ref[rs] = new
        if n_ref is not None:
            n_ref[rs] = layer_norm(new, gain_ref[...], bias_ref[...])

    for ring in range(RINGS):
        for sub in range(SUBS):
            done = acc.at[ring, sub, pl.ds(0, last)]
            pltpu.make_async_copy(done, done, send_sem.at[ring, sub]).wait()


def reduce_layer(torus, layer, from_normed, last_layer, source, ctxs, w_outs, w_downs, w_ups, residual, gain, bias):
    rows, d_model = residual.shape
    heads, cols = ctxs[0].shape[2], w_downs[0].shape[1]
    depth = CORES * (heads + cols)
    share = rows // RINGS
    anys = [pl.BlockSpec(memory_space=pl.ANY)] * 9
    vmem = pl.BlockSpec(memory_space=pltpu.VMEM)
    n_out = 1 if last_layer else 2
    return pl.pallas_call(
        functools.partial(reduce_kernel, torus, layer, from_normed, last_layer),
        name=f"reduce_layer_{layer}",
        out_shape=[jax.ShapeDtypeStruct((rows, d_model), BF16)] * n_out,
        in_specs=[*anys, vmem, vmem, vmem],
        out_specs=[vmem] * n_out,
        scratch_shapes=[
            pltpu.VMEM((torus.chips, rows, CORES * heads), BF16),
            pltpu.VMEM((depth, d_model), BF16),
            pltpu.VMEM((d_model, CORES * cols) if from_normed else (16, 128), BF16),
            pltpu.VMEM((2, rows, source.shape[2]), BF16),
            pltpu.VMEM((rows, depth), BF16),
            pltpu.VMEM((rows, d_model), F32),
            pltpu.VMEM((RINGS, SUBS, torus.chips, share, d_model // SUBS), BF16),
            pltpu.SemaphoreType.DMA((8,)),
            pltpu.SemaphoreType.DMA((2, RINGS)),
            pltpu.SemaphoreType.DMA((RINGS, SUBS)),
            pltpu.SemaphoreType.DMA((RINGS, SUBS, torus.chips - 1)),
        ],
        compiler_params=pltpu.CompilerParams(collective_id=3 + layer, has_side_effects=True, vmem_limit_bytes=VMEM_LIMIT),
    )(source, *ctxs, *w_outs, *w_downs, *w_ups, residual, gain.reshape(1, -1), bias.reshape(1, -1))


def project_kernel(torus, layer, n_ref, wq0, wq1, wu0, wu1, qkv_ref, up_ref, w_buf, got, stage, load_sem, send_sem, recv_sem):
    core, x, y = torus.me()
    pos = [torus.position(ring, x, y) for ring in range(RINGS)]
    rows = n_ref.shape[0]
    share = rows // RINGS
    last = torus.chips - 1
    copies = []
    start = 0
    for i, w_src in enumerate((wq0, wq1, wu0, wu1)):
        width = w_src.shape[2]
        copies.append(pltpu.make_async_copy(w_src.at[layer], w_buf.at[:, pl.ds(start, width)], load_sem.at[i]))
        start += width
    own_chip = y * torus.side + x
    own = pltpu.make_async_copy(n_ref, got.at[own_chip], load_sem.at[4])
    own.start()
    for copy in copies:
        copy.start()
    nexts = enter(torus, core, pos)
    own.wait()

    def block(ring, step):
        return torus.chip_at(ring, pos[ring] - torus.sign(ring) * step)

    def piece(ring, step):
        return got.at[block(ring, step), pl.ds(ring * share, share)]

    def send(ring, step):
        return pltpu.make_async_remote_copy(
            src_ref=piece(ring, step), dst_ref=piece(ring, step), send_sem=send_sem.at[ring],
            recv_sem=recv_sem.at[ring, step], device_id={"tp": nexts[ring]}, device_id_type=MESH_ID)

    def arrived(ring, step):
        return pltpu.make_async_remote_copy(
            src_ref=piece(ring, step + 1), dst_ref=piece(ring, step + 1), send_sem=send_sem.at[ring],
            recv_sem=recv_sem.at[ring, step], device_id={"tp": nexts[ring]}, device_id_type=MESH_ID)

    tile = 256

    def compute(step):
        for ring in range(RINGS):
            stage[pl.ds(ring * share, share)] = got[block(ring, step), pl.ds(ring * share, share)]

        @pl.loop(0, qkv_ref.shape[2] // tile)
        def _(j):
            cs = pl.ds(pl.multiple_of(j * tile, tile), tile)
            res = jnp.dot(stage[...], w_buf[:, cs], preferred_element_type=F32)
            for ring in range(RINGS):
                rs = slice(ring * share, (ring + 1) * share)
                qkv_ref[block(ring, step), rs, cs] = res[rs]

        @pl.loop(0, up_ref.shape[2] // tile)
        def _(j):
            off = pl.multiple_of(j * tile, tile)
            res = jnp.dot(stage[...], w_buf[:, pl.ds(pl.multiple_of(qkv_ref.shape[2] + off, tile), tile)], preferred_element_type=F32)
            act = gelu(res).astype(BF16)
            for ring in range(RINGS):
                rs = slice(ring * share, (ring + 1) * share)
                up_ref[block(ring, step), rs, pl.ds(off, tile)] = act[rs]

    for ring in range(RINGS):
        send(ring, 0).start()
    for copy in copies:
        copy.wait()
    compute(0)

    @pl.loop(1, last)
    def _(step):
        for ring in range(RINGS):
            arrived(ring, step - 1).wait_recv()
            send(ring, step).start()
        compute(step)

    for ring in range(RINGS):
        arrived(ring, last - 1).wait_recv()
    compute(last)
    for ring in range(RINGS):
        done = got.at[pl.ds(0, last), pl.ds(ring * share, share)]
        pltpu.make_async_copy(done, done, send_sem.at[ring]).wait()


def gather_project(torus, layer, normed, w_qkvs, w_ups):
    rows, d_model = normed.shape
    n_qkv, n_up = CORES * w_qkvs[0].shape[2], CORES * w_ups[0].shape[2]
    width = n_qkv + n_up
    anys = [pl.BlockSpec(memory_space=pl.ANY)] * 5
    return pl.pallas_call(
        functools.partial(project_kernel, torus, layer),
        name="gather_project",
        out_shape=[jax.ShapeDtypeStruct((torus.chips, rows, n_qkv), F32), jax.ShapeDtypeStruct((torus.chips, rows, n_up), BF16)],
        in_specs=anys,
        out_specs=[pl.BlockSpec(memory_space=pltpu.VMEM)] * 2,
        scratch_shapes=[
            pltpu.VMEM((d_model, width), BF16),
            pltpu.VMEM((torus.chips, rows, d_model), BF16),
            pltpu.VMEM((rows, d_model), BF16),
            pltpu.SemaphoreType.DMA((5,)),
            pltpu.SemaphoreType.DMA((RINGS,)),
            pltpu.SemaphoreType.DMA((RINGS, torus.chips - 1)),
        ],
        compiler_params=pltpu.CompilerParams(collective_id=1, has_side_effects=True, vmem_limit_bytes=VMEM_LIMIT),
    )(normed, *w_qkvs, *w_ups)


def gather_kernel(torus, y_ref, out_ref, got, load_sem, send_sem, recv_sem, pair_sem, store_sem):
    core, x, y = torus.me()
    pos = [torus.position(ring, x, y) for ring in range(RINGS)]
    rows = y_ref.shape[0]
    share = rows // RINGS
    last = torus.chips - 1
    own_chip = y * torus.side + x
    own = pltpu.make_async_copy(y_ref, got.at[own_chip], load_sem.at[0])
    own.start()
    partner = own_chip * CORES + (CORES - 1 - core)
    nexts = enter(torus, core, pos, (partner,))
    own.wait()

    def block(ring, step):
        return torus.chip_at(ring, pos[ring] - torus.sign(ring) * step)

    thin = share // SUBS

    def piece(ring, sub, step):
        return got.at[block(ring, step), pl.ds(ring * share + sub * thin, thin)]

    def send(ring, sub, step):
        return pltpu.make_async_remote_copy(
            src_ref=piece(ring, sub, step), dst_ref=piece(ring, sub, step), send_sem=send_sem.at[ring, sub],
            recv_sem=recv_sem.at[ring, sub, step], device_id={"tp": nexts[ring]}, device_id_type=MESH_ID)

    def arrived(ring, sub, step):
        return pltpu.make_async_remote_copy(
            src_ref=piece(ring, sub, step + 1), dst_ref=piece(ring, sub, step + 1), send_sem=send_sem.at[ring, sub],
            recv_sem=recv_sem.at[ring, sub, step], device_id={"tp": nexts[ring]}, device_id_type=MESH_ID)

    def spread(ring, step):
        src = got.at[block(ring, step), pl.ds(ring * share, share)]
        dst = out_ref.at[core * torus.chips + block(ring, step), pl.ds(ring * share, share)]
        pltpu.make_async_remote_copy(
            src_ref=src, dst_ref=dst, send_sem=pair_sem.at[0], recv_sem=pair_sem.at[1],
            device_id={"tp": partner}, device_id_type=MESH_ID).start()
        pltpu.make_async_copy(src, dst, store_sem.at[0]).start()

    for sub in range(SUBS):
        for ring in range(RINGS):
            send(ring, sub, 0).start()
    for ring in range(RINGS):
        spread(ring, 0)

    @pl.loop(1, last)
    def _(step):
        for sub in range(SUBS):
            for ring in range(RINGS):
                arrived(ring, sub, step - 1).wait_recv()
                send(ring, sub, step).start()
        for ring in range(RINGS):
            spread(ring, step)

    for ring in range(RINGS):
        for sub in range(SUBS):
            arrived(ring, sub, last - 1).wait_recv()
        spread(ring, last)
    for ring in range(RINGS):
        for sub in range(SUBS):
            done = got.at[pl.ds(0, last), pl.ds(ring * share + sub * thin, thin)]
            pltpu.make_async_copy(done, done, send_sem.at[ring, sub]).wait()
    pltpu.make_async_copy(got, got, pair_sem.at[0]).wait()
    pltpu.make_async_copy(got, got, store_sem.at[0]).wait()
    pltpu.make_async_copy(got, got, pair_sem.at[1]).wait()


def gather_all(torus, y_own):
    rows, d_model = y_own.shape
    return pl.pallas_call(
        functools.partial(gather_kernel, torus),
        name="gather_all",
        out_shape=jax.ShapeDtypeStruct((CORES * torus.chips, rows, d_model), BF16),
        in_specs=[pl.BlockSpec(memory_space=pl.ANY)],
        out_specs=pl.BlockSpec(memory_space=pl.ANY),
        scratch_shapes=[
            pltpu.VMEM((torus.chips, rows, d_model), BF16),
            pltpu.SemaphoreType.DMA((1,)),
            pltpu.SemaphoreType.DMA((RINGS, SUBS)),
            pltpu.SemaphoreType.DMA((RINGS, SUBS, torus.chips - 1)),
            pltpu.SemaphoreType.DMA((2,)),
            pltpu.SemaphoreType.DMA((1,)),
        ],
        compiler_params=pltpu.CompilerParams(collective_id=2, has_side_effects=True, vmem_limit_bytes=VMEM_LIMIT),
    )(y_own)


def solution(mesh):
    n_tp = mesh.shape["tp"]
    torus = Torus(math.isqrt(n_tp // CORES))
    swap = [(i, i ^ 1) for i in range(n_tp)]

    def shard_body(act_in, ln_gain, ln_bias, w_qkv, w_out, w_up, w_down):
        layers = ln_gain.shape[0]
        head_dim = w_out.shape[1]
        idx = lax.axis_index("tp")
        core, chip = lax.rem(idx, CORES), lax.div(idx, CORES)
        w_qkv = w_qkv[:, :, 0]
        w_qkvs, w_ups, w_outs, w_downs = [(w, lax.ppermute(w, "tp", swap)) for w in (w_qkv, w_up, w_out, w_down)]

        half = lax.dynamic_slice_in_dim(act_in, core * torus.chips, torus.chips, 0)
        own = lax.dynamic_index_in_dim(half, chip, 0, keepdims=False)
        normed = layer_norm(half, ln_gain[0], ln_bias[0])
        for layer in range(layers):
            if layer == 0:
                source = normed
                qkvs = [jnp.einsum("bsd,dc->bsc", normed, w[layer], preferred_element_type=F32) for w in w_qkvs]
            else:
                qkv, source = gather_project(torus, layer, normed, w_qkvs, w_ups)
                n_qkv = w_qkv.shape[2]
                qkvs = [qkv[..., i * n_qkv:(i + 1) * n_qkv] for i in range(CORES)]
            ctxs = [attend(qkv, head_dim) for qkv in qkvs]
            nxt = (layer + 1) % layers
            outs = reduce_layer(torus, layer, layer == 0, layer == layers - 1, source, ctxs, w_outs, w_downs, w_ups, own, ln_gain[nxt], ln_bias[nxt])
            own, normed = outs[0], outs[-1]
        return gather_all(torus, own)

    return jax.shard_map(shard_body, mesh=mesh, in_specs=(P("dp", None, None), P(None, None), P(None, None), P(None, None, "tp", None), P(None, "tp", None), P(None, None, "tp"), P(None, "tp", None)), out_specs=P("dp", None, None), check_vma=False)
```

time: 688 us -> 532 us (0.77)
  Pallas kernels: 478 us -> 416 us
  matrix products: 93.9 us -> 43.5 us
  other arithmetic: 55.5 us -> 37.3 us
  local copies, waits for them, and re-layouts: 46.5 us -> 29 us
    dot_general x4 -> x2, matrix products: 72.3 us -> 20.2 us  [shard_body(): jnp.einsum('bsd,dc->bsc', normed, w[layer], preferred_element_type=F32)]
    pallas_call x1, Pallas kernels: 142 us -> 109 us  [gather_all(): pl.pallas_call(functools.partial(gather_kernel, torus), name='gather_all'...]
    pallas_call x3, Pallas kernels: 336 us -> 307 us  [the longest x2 197 us: reduce_layer(): pl.pallas_call(functools.partial(reduce_kernel, torus, layer, from_normed...]
    squeeze x4 -> x0, local copies, waits for them, and re-layouts: 19.8 us -> none  [shard_body(): w[layer]]
    another operation x3, other arithmetic: 18.8 us -> 10.2 us
    convert_element_type x1, other arithmetic: 20.4 us -> 12.1 us  [layer_norm(): return (centered * lax.rsqrt(row_var + LN_EPS) * gain + bias).astype(BF16)]
    unnamed x53 -> x19, local copies, waits for them, and re-layouts: 23.6 us -> 25.9 us
  transfers between devices with their start and end apart: 8 -> 4, of which waited for: 0 -> 0; matrix products, arithmetic and copies ran while one was open for 25% -> 12% of each run, Pallas kernels for 33% -> 0%
where the time goes in v2:
time: 532 us; the launch traced here: 529 us
  Pallas kernels  416 us (78%)
  matrix products  43.5 us (8%)
  other arithmetic  37.3 us (7%)
  local copies, waits for them, and re-layouts  29 us (5%)
    pallas_call x2, Pallas kernels, reduce_layer(): pl.pallas_call(functools.partial(reduce_kernel, torus, layer, from_normed...  197 us
    pallas_call x1, Pallas kernels, gather_project(): pl.pallas_call(functools.partial(project_kernel, torus, layer), name='gat...  110 us
    pallas_call x1, Pallas kernels, gather_all(): pl.pallas_call(functools.partial(gather_kernel, torus), name='gather_all'...  109 us
    unnamed x19, local copies, waits for them, and re-layouts  25.9 us
    dot_general x2, matrix products, shard_body(): jnp.einsum('bsd,dc->bsc', normed, w[layer], preferred_element_type=F32)  20.2 us
    convert_element_type x1, other arithmetic, layer_norm(): return (centered * lax.rsqrt(row_var + LN_EPS) * gain + bias).astype(BF16)  12.1 us
    dot_general x4, matrix products, attend(): jnp.einsum('bst,btd->bsd', probs, values, preferred_element_type=F32)  11.9 us
    sub x4, matrix products, attend(): probs = jax.nn.softmax(scores, axis=-1).astype(BF16)  11.4 us
  transfers between devices with their start and end apart: 4, of which 0 were waited for; matrix products, arithmetic and copies ran while one was open for 12% of the time, Pallas kernels for 0%

profile of v2, /device:TPU:97, one launch (start us, length us, event | category | flops | bytes accessed | tf_op | source)
XLA Modules:
  0.0 528.8 jit_solution(12354152185459324156)
XLA Ops:
  0.0 2.0 collective-permute-start.1
  2.0 0.5 collective-permute-start.2
  2.5 0.0 collective-permute-start.3
  2.5 6.9 %convert_reduce_fusion = f32[16,128]{1,0:T(8,128)S(1)} fusion(bf16[32,128,4096]{2,1,0:T(8,128)(2,1)} %param.7, s32[]{:T(128)S(6)} %select_n.24), kind=kLoop, calls=%fused_computation.5 | loop fusion | flops 16775168 | bytes 16785412 | tf_op jit(solution)/shard_map/reduce_sum | solution.py:24
  9.4 0.0 copy-start.5
  9.4 0.0 copy-start.6
  9.4 7.9 %fusion.6 = f32[16,128]{1,0:T(8,128)S(1)} fusion(f32[16,128]{1,0:T(8,128)S(1)} %broadcast_multiply_fusion, bf16[32,128,4096]{2,1,0:T(8,128)(2,1)} %param.7, s32[]{:T(128)S(6)} %select_n.24), kind=kLoop, calls=%fused_computation.8 | loop fusion | flops 33552384 | bytes 16793604 | tf_op jit(solution)/shard_map/reduce_sum | solution.py:26
  17.4 0.3 fusion.73
  17.7 0.7 fusion.146
  18.3 2.4 dynamic-slice_bitcast_fusion.refs_9_
  20.8 12.1 %fusion.9.refs_0_ = bf16[16,128,4096]{2,1,0:T(8,128)(2,1)S(1)} fusion(f32[4096]{0:T(1024)S(1)} %bitcast.20, f32[4096]{0:T(1024)S(1)} %bitcast.21, f32[16,128]{1,0:T(8,128)S(1)} %add_rsqrt_fusion, f32[16,128]{1,0:T(8,128)S(1)} %broadcast_multiply_fusion, bf16[32,128,4096]{2,1,0:T(8,128)(2,1)} %param.7, s32[]{:T(128)S(6)} %select_n.24), kind=kLoop, calls=%fused_computation.11 | loop fusion | flops 50331648 | bytes 33603588 | tf_op jit(solution)/shard_map/convert_element_type | solution.py:27
  32.9 0.0 copy-start
  32.9 9.2 %fusion.11 = f32[16,128,384]{2,1,0:T(8,128)S(1)} fusion(bf16[16,128,4096]{2,1,0:T(8,128)(2,1)S(1)} %fusion.9.refs_0_, bf16[2,4096,1,384]{3,1,2,0:T(8,128)(2,1)S(1)} %bitcast.19), kind=kOutput, calls=%fused_computation.14 | convolution fusion | flops 6442450944 | bytes 23068672 | tf_op jit(solution)/shard_map/bsd,dc->bsc/dot_general | solution.py:457
  42.1 11.0 %fusion.10 = f32[16,128,384]{2,1,0:T(8,128)S(1)} fusion(bf16[16,128,4096]{2,1,0:T(8,128)(2,1)S(1)} %fusion.9.refs_0_, bf16[2,4096,384]{2,1,0:T(8,128)(2,1)} %collective-permute-done.wq1), kind=kOutput, calls=%fused_computation.13 | convolution fusion | flops 6442450944 | bytes 23068672 | tf_op jit(solution)/shard_map/bsd,dc->bsc/dot_general | solution.py:457
  53.2 1.7 copy-done.2
  54.9 3.5 subtract_convert_fusion.4
  58.4 2.4 fusion.153
  60.7 2.4 fusion.148
  63.1 3.8 convolution_convert_fusion.2.refs_2_
  66.9 3.4 convolution_convert_fusion.3.refs_1_
  70.3 106.3 %reduce_layer_0.1 = (bf16[128,4096]{1,0:T(8,128)(2,1)}, bf16[128,4096]{1,0:T(8,128)(2,1)}) custom-call(bf16[16,128,4096]{2,1,0:T(8,128)(2,1)} %copy-done, bf16[16,128,128]{2,1,0:T(8,128)(2,1)} %convolution_convert_fusion.3.refs_1_, bf16[16,128,128]{2,1,0:T(8,128)(2,1)} %convolution_convert_fusion.2.refs_2_, bf16[2,128,4096]{2,1,0:T(8,128)(2,1)} %refs_3_.3, ...), custom_call_target="tpu_custom_call" | custom-call | tf_op jit(solution)/shard_map/reduce_layer_0/pallas_call | solution.py:225
  176.6 110.2 %gather_project.1 = (f32[16,128,768]{2,1,0:T(8,128)}, bf16[16,128,1024]{2,1,0:T(8,128)(2,1)}) custom-call(bf16[128,4096]{1,0:T(8,128)(2,1)} %get-tuple-element.9.n_ref, bf16[2,4096,384]{2,1,0:T(8,128)(2,1)} %bitcast.17, bf16[2,4096,384]{2,1,0:T(8,128)(2,1)} %collective-permute-done.wq1, bf16[2,4096,512]{2,1,0:T(8,128)(2,1)} %refs_7_.3, ...), custom_call_target="tpu_custom_call" | custom-call | tf_op jit(solution)/shard_map/gather_project/pallas_call | solution.py:333
  286.8 3.3 convert.72
  290.1 1.3 copy-done.1
  291.4 3.4 subtract_convert_fusion
  294.8 3.3 fusion.158
  298.1 2.4 convolution_convert_fusion.1.refs_1_
  300.5 3.3 fusion.163
  303.8 2.4 convolution_convert_fusion.refs_2_
  306.2 90.7 %reduce_layer_1.1.y_ref = bf16[128,4096]{1,0:T(8,128)(2,1)} custom-call(bf16[16,128,1024]{2,1,0:T(8,128)(2,1)} %get-tuple-element.10.refs_0_, bf16[16,128,128]{2,1,0:T(8,128)(2,1)} %convolution_convert_fusion.1.refs_1_, bf16[16,128,128]{2,1,0:T(8,128)(2,1)} %convolution_convert_fusion.refs_2_, bf16[2,128,4096]{2,1,0:T(8,128)(2,1)} %refs_3_.3, ...), custom_call_target="tpu_custom_call" | custom-call | tf_op jit(solution)/shard_map/reduce_layer_1/pallas_call | solution.py:225
  396.9 108.5 %gather_all.1 = bf16[32,128,4096]{2,1,0:T(8,128)(2,1)} custom-call(bf16[128,4096]{1,0:T(8,128)(2,1)} %reduce_layer_1.1.y_ref), custom_call_target="tpu_custom_call" | custom-call | tf_op jit(solution)/shard_map/gather_all/pallas_call | solution.py:420
  505.4 22.9 %copy.17 = bf16[32,128,4096]{2,1,0:T(8,128)(2,1)} copy(bf16[32,128,4096]{2,1,0:T(8,128)(2,1)} %gather_all.1) | data formatting | bytes 67108864
  (23 shorter events, 0.1 us)
Async XLA Ops:
  0.0 70.2 %collective-permute-start.1 = (bf16[2,128,4096]{2,1,0:T(8,128)(2,1)}, bf16[2,128,4096]{2,1,0:T(8,128)(2,1)}, u32[]{:S(2)}, u32[]{:S(2)}) collective-permute-start(bf16[2,128,4096]{2,1,0:T(8,128)(2,1)} %refs_3_.3), channel_id=1, source_target_pairs={{0,1},{1,0},{2,3},{3,2},{4,5},{5,4},{6,7},{7,6},{8,9},{9,8},{10,11... | collective-permute-start | bytes 6291464 | tf_op jit(solution)/shard_map/ppermute | solution.py:449
  2.0 40.1 %collective-permute-start = (bf16[2,4096,384]{2,1,0:T(8,128)(2,1)}, bf16[2,4096,384]{2,1,0:T(8,128)(2,1)}, u32[]{:S(2)}, u32[]{:S(2)}) collective-permute-start(bf16[2,4096,384]{2,1,0:T(8,128)(2,1)} %bitcast.16), channel_id=1, source_target_pairs={{0,1},{1,0},{2,3},{3,2},{4,5},{5,4},{6,7},{7,6},{8,9},{9,8},{10,11... | collective-permute-start | bytes 18874376 | tf_op jit(solution)/shard_map/ppermute | solution.py:449
  2.0 68.2 %collective-permute-start.2 = (bf16[2,512,4096]{2,1,0:T(8,128)(2,1)}, bf16[2,512,4096]{2,1,0:T(8,128)(2,1)}, u32[]{:S(2)}, u32[]{:S(2)}) collective-permute-start(bf16[2,512,4096]{2,1,0:T(8,128)(2,1)} %refs_5_.3), channel_id=1, source_target_pairs={{0,1},{1,0},{2,3},{3,2},{4,5},{5,4},{6,7},{7,6},{8,9},{9,8},{10,11... | collective-permute-start | bytes 25165832 | tf_op jit(solution)/shard_map/ppermute | solution.py:449
  2.5 67.7 %collective-permute-start.3 = (bf16[2,4096,512]{2,1,0:T(8,128)(2,1)}, bf16[2,4096,512]{2,1,0:T(8,128)(2,1)}, u32[]{:S(2)}, u32[]{:S(2)}) collective-permute-start(bf16[2,4096,512]{2,1,0:T(8,128)(2,1)} %refs_7_.3), channel_id=1, source_target_pairs={{0,1},{1,0},{2,3},{3,2},{4,5},{5,4},{6,7},{7,6},{8,9},{9,8},{10,11... | collective-permute-start | bytes 25165832 | tf_op jit(solution)/shard_map/ppermute | solution.py:449
  9.4 8.2 %copy-start.5 = (f32[2,4096]{1,0:T(2,128)S(1)}, f32[2,4096]{1,0:T(2,128)}, u32[]{:S(2)}) copy-start(f32[2,4096]{1,0:T(2,128)} %param.9) | copy-start | bytes 98308
  9.4 8.2 %copy-start.6 = (f32[2,4096]{1,0:T(2,128)S(1)}, f32[2,4096]{1,0:T(2,128)}, u32[]{:S(2)}) copy-start(f32[2,4096]{1,0:T(2,128)} %param.8) | copy-start | bytes 98308
  18.3 14.5 %copy-start.3 = (f32[1,4096]{1,0:T(1,128)}, f32[1,4096]{1,0:T(1,128)S(1)}, u32[]{:S(2)}) copy-start(f32[1,4096]{1,0:T(1,128)S(1)} %get-tuple-element.34.refs_11_) | copy-start | bytes 49156
  18.3 14.5 %copy-start.4 = (f32[1,4096]{1,0:T(1,128)}, f32[1,4096]{1,0:T(1,128)S(1)}, u32[]{:S(2)}) copy-start(f32[1,4096]{1,0:T(1,128)S(1)} %get-tuple-element.43.refs_10_) | copy-start | bytes 49156
  18.3 14.5 %slice-start = ((s8[6291456]{0:T(1024)(128)(4,1)}), s8[4194304]{0:T(1024)(128)(4,1)S(1)}, s32[]{:S(2)}) async-start(s8[6291456]{0:T(1024)(128)(4,1)} %bitcast.18), calls=%async_computation | async-start | bytes 8388608
  20.8 12.1 %slice-start.1 = ((s8[6291456]{0:T(1024)(128)(4,1)}), s8[2097152]{0:T(1024)(128)(4,1)S(1)}, s32[]{:S(2)}) async-start(s8[6291456]{0:T(1024)(128)(4,1)} %bitcast.18), calls=%async_computation.1 | async-start | bytes 4194304
  32.9 9.2 %copy-start = (bf16[16,128,4096]{2,1,0:T(8,128)(2,1)}, bf16[16,128,4096]{2,1,0:T(8,128)(2,1)S(1)}, u32[]{:S(2)}) copy-start(bf16[16,128,4096]{2,1,0:T(8,128)(2,1)S(1)} %fusion.9.refs_0_) | copy-start | bytes 50331652
  53.2 1.7 copy-start.2
  286.8 4.6 copy-start.1
